TPU v7x, 32 devices: a whole 2x2x4 slice. The times are simulated.
32 devices in a mesh: grp: 2 (over y), gx: 4 (over z), gy: 2 (over x), gz: 2 (over core).
Axes of the slice: x: 2, y: 2, z: 4, core: 2. Of those that a mesh axis runs over, the one named last changes fastest.
Arguments:
- observed: float32 [2048, 4, 256], P(('grp', 'gx', 'gy', 'gz')), parts along dimension 0, may hold values from -12 to 12
- predicted: float32 [2048, 4, 256], P(('grp', 'gx', 'gy', 'gz')), parts along dimension 0, may hold values from -6 to 6
- coherence_mask: int32 [2048, 256], P(('grp', 'gx', 'gy', 'gz')), parts along dimension 0, may hold values 0 or 1
- block_count: int32 [2048], P(('grp', 'gx', 'gy', 'gz')), parts along dimension 0, may hold values from 64 to 256
- block_owner: int32 [2048, 1], P(('grp', 'gx', 'gy', 'gz')), parts along dimension 0, may hold values from 0 to 7; in each aligned block of 64 rows (0 to 63, 64 to 127, ...) at most 16 rows name the same one
- block_matrix_choice: int32 [2048], P(('grp', 'gx', 'gy', 'gz')), parts along dimension 0, may hold values from 0 to 31
- block_patch: int32 [2048], P(('grp', 'gx', 'gy', 'gz')), parts along dimension 0, may hold values from 0 to 31
- look_vector: float32 [4, 3], replicated, may hold values from -1 to 1
- interp_weights: bfloat16 [32, 256, 128], replicated, may hold values from -0.375 to 0.375
- depth_kernel: float32 [64], P(('grp', 'gz')), parts along dimension 0, may hold values from 0.2 to 1
- stiffness: float32 [64, 128, 256], P(('grp', 'gz'), 'gx', 'gy'), parts along dimension 0, may hold values from 0.25 to 4
Outputs:
- adjoint_field: float32 [3, 64, 128, 256], P(None, ('grp', 'gz'), 'gx', 'gy'), parts along dimension 1
- cg_residual: float32 [3, 64, 128, 256], P(None, ('grp', 'gz'), 'gx', 'gy'), parts along dimension 1
There are 2 independent parts, one for each index of `grp`. A program takes and returns all parts, laid end to end along the dimension named above; an argument that names none is the same for every part. Nothing has to cross between parts.
Inputs may be any that keep to these rules, and one draw needn't show every extreme that they name: `block_owner`: the blocks of one device name no column tile more than 16 times; in some devices one tile is named exactly 16 times.
All inputs are finite; a program needn't handle non-finite values. No bound on the sum of `coherence_mask` on one device may be relied on, other than what follows from the above.
Results may differ from a plain program's by a relative error of at most 0.0029.
Values sent between devices are 32-bit elements; how exact they have to be, the bound alone decides.
A program may use at most 64 MiB of HBM per device.

v0:
```python
import math

import jax
import jax.numpy as jnp
from jax import lax
from jax.sharding import PartitionSpec as P

EPOCHS = 4
PATCH_X = 8
PATCH_Y = 16
ITERS = 3


KAPPA = 0.5
EPS = 1e-06
SPATIAL = (1, 2, 0)


def extended(cells, sides, width):
    for axis, dim in sides:
        count = lax.axis_size(axis)
        ends = count - 1
        head = lax.slice_in_dim(cells, 0, width, axis=dim)
        tail = lax.slice_in_dim(cells, cells.shape[dim] - width, cells.shape[dim], axis=dim)
        cells = jnp.concatenate(
            [
                lax.ppermute(tail, axis, [(i, (i + 1) % count) for i in range(ends)]),
                cells,
                lax.ppermute(head, axis, [((i + 1) % count, i) for i in range(ends)]),
            ],
            axis=dim,
        )
    return cells


def beside_all(padded):
    total = padded[2:, 1:-1, 1:-1] + padded[:-2, 1:-1, 1:-1]
    total = total + padded[1:-1, 2:, 1:-1] + padded[1:-1, :-2, 1:-1]
    return total + padded[1:-1, 1:-1, 2:] + padded[1:-1, 1:-1, :-2]


def central(padded, axis):
    if axis == 0:
        return 0.5 * (padded[2:, 1:-1, 1:-1] - padded[:-2, 1:-1, 1:-1])
    if axis == 1:
        return 0.5 * (padded[1:-1, 2:, 1:-1] - padded[1:-1, :-2, 1:-1])
    return 0.5 * (padded[1:-1, 1:-1, 2:] - padded[1:-1, 1:-1, :-2])


def operate(field, stiffness):
    padded = extended(field, (("gx", 2), ("gy", 3), ("gz", 1)), 1)
    spread = (
        central(padded[0], SPATIAL[0])
        + central(padded[1], SPATIAL[1])
        + central(padded[2], SPATIAL[2])
    )
    spread_pad = extended(spread, (("gx", 1), ("gy", 2), ("gz", 0)), 1)
    parts = [
        (6.0 + stiffness) * field[member]
        - beside_all(padded[member])
        - KAPPA * central(spread_pad, SPATIAL[member])
        for member in range(3)
    ]
    return jnp.stack(parts)


def project(resid, look_vector):
    return jnp.einsum("ec,nep->ncp", look_vector, resid, precision=lax.Precision.HIGHEST).astype(
        jnp.bfloat16
    )


def contribute(coeffs, tables, weights):
    total = coeffs.shape[0]
    group = math.gcd(total, 32)
    coefficient_sets = coeffs.reshape(total // group, group, 3, coeffs.shape[2])
    table_groups = tables.reshape(total // group, group)

    def per_group(both_parts):
        block_coefficient_values, block_tables = both_parts
        selected_entries = jnp.take(weights, block_tables, axis=0)
        return jnp.einsum(
            "aow,awv->aov",
            block_coefficient_values,
            selected_entries,
            preferred_element_type=jnp.float32,
        )

    result = lax.map(per_group, (coefficient_sets, table_groups))
    return result.reshape(total, 3, weights.shape[2])


def two_products(residual, image):
    return lax.psum((jnp.sum(residual * residual), jnp.sum(residual * image)), ("gx", "gy", "gz"))


def per_device(
    observed,
    predicted,
    coherence_mask,
    block_count,
    block_owner,
    block_matrix_choice,
    block_patch,
    look_vector,
    interp_weights,
    depth_kernel,
    stiffness,
):
    blocks = observed.shape[0]
    pixels = observed.shape[2]
    cells = PATCH_X * PATCH_Y
    owners = lax.axis_size("gx") * lax.axis_size("gy")
    capacity = max(4, 2 * blocks // owners)
    slots = owners * capacity
    local_x = stiffness.shape[1]
    local_y = stiffness.shape[2]
    places_x = local_x // PATCH_X
    northing_places = local_y // PATCH_Y
    places = places_x * northing_places
    column = lax.broadcasted_iota(jnp.int32, (blocks, pixels), 1)
    valid = coherence_mask.astype(jnp.float32) * (column < block_count[:, None]).astype(jnp.float32)
    resid = (predicted - observed) * valid[:, None, :]
    misfit, weight = lax.psum((jnp.sum(resid * resid), jnp.sum(valid)), ("gx", "gy", "gz"))
    scale = lax.rsqrt(misfit / (EPOCHS * weight) + EPS)
    owner = block_owner[:, 0]
    order = lax.broadcasted_iota(jnp.int32, (blocks, blocks), 0)
    other = lax.broadcasted_iota(jnp.int32, (blocks, blocks), 1)
    earlier = (owner[:, None] == owner[None, :]) & (other < order)
    rank = jnp.sum(earlier.astype(jnp.int32), axis=1)
    slot = owner * capacity + rank
    slot_ids = lax.broadcasted_iota(jnp.int32, (blocks, slots), 1)
    chosen = slot_ids == slot[:, None]
    select = chosen.astype(jnp.float32)
    patch_slot = jnp.sum(jnp.where(chosen, block_patch[:, None], 0), axis=0).reshape(
        owners, capacity
    )
    table_slot = jnp.sum(jnp.where(chosen, block_matrix_choice[:, None], 0), axis=0).reshape(
        owners, capacity
    )
    resid_slot = jnp.einsum("bs,bep->sep", select, resid, precision=lax.Precision.HIGHEST).reshape(
        owners, capacity, EPOCHS, pixels
    )
    arrived = lax.all_to_all(resid_slot, ("gx", "gy"), split_axis=0, concat_axis=0, tiled=True)
    tables = lax.all_to_all(table_slot, ("gx", "gy"), split_axis=0, concat_axis=0, tiled=True)
    patches = lax.all_to_all(patch_slot, ("gx", "gy"), split_axis=0, concat_axis=0, tiled=True)
    sources = tables.shape[0]
    width = tables.shape[1]
    coeffs = project(arrived.reshape(sources * width, EPOCHS, pixels), look_vector)
    sums = contribute(coeffs, tables.reshape(sources * width), interp_weights)
    patch_total_sums = sums.reshape(sources, width, 3, cells)
    flat_sums = patch_total_sums.reshape(slots, 3, cells)
    flat_ids = patches.reshape(slots)
    place_ids = lax.broadcasted_iota(jnp.int32, (slots, places), 1)
    onehot = (flat_ids[:, None] == place_ids).astype(jnp.float32)
    placed = jnp.einsum("np,ncs->pcs", onehot, flat_sums, precision=lax.Precision.HIGHEST)
    surface = (
        placed.reshape(places_x, northing_places, 3, PATCH_X, PATCH_Y)
        .transpose(2, 0, 3, 1, 4)
        .reshape(3, local_x, local_y)
    )
    surface = lax.psum(surface, "gz")
    source = scale * depth_kernel[None, :, None, None] * surface[:, None, :, :]
    adjoint_field = jnp.zeros_like(source)
    cg_residual = source
    image = operate(cg_residual, stiffness)
    norm_now, product = two_products(cg_residual, image)
    alpha = norm_now / product
    direction = cg_residual
    along = image
    for step in range(ITERS):
        adjoint_field = adjoint_field + alpha * direction
        cg_residual = cg_residual - alpha * along
        if step + 1 < ITERS:
            image = operate(cg_residual, stiffness)
            norm_next, product = two_products(cg_residual, image)
            ratio = norm_next / norm_now
            alpha = norm_next / (product - ratio * norm_next / alpha)
            direction = cg_residual + ratio * direction
            along = image + ratio * along
            norm_now = norm_next
    return (adjoint_field, cg_residual)


def solution(mesh):
    in_specs = (
        P(("grp", "gx", "gy", "gz"), None, None),
        P(("grp", "gx", "gy", "gz"), None, None),
        P(("grp", "gx", "gy", "gz"), None),
        P(("grp", "gx", "gy", "gz")),
        P(("grp", "gx", "gy", "gz"), None),
        P(("grp", "gx", "gy", "gz")),
        P(("grp", "gx", "gy", "gz")),
        P(),
        P(),
        P(("grp", "gz")),
        P(("grp", "gz"), "gx", "gy"),
    )
    out_specs = (P(None, ("grp", "gz"), "gx", "gy"), P(None, ("grp", "gz"), "gx", "gy"))
    return jax.shard_map(
        per_device, mesh=mesh, in_specs=in_specs, out_specs=out_specs, check_vma=False
    )
```

profile of v0, /device:TPU:0, one launch (start us, length us, event | category | flops | bytes accessed | tf_op | source)
XLA Modules:
  0.0 349.5 jit_solution(3229247939557360916)
XLA Ops:
  3.7 7.3 %all-to-all-start.2 = ((s32[8,1,16]{2,1,0:T(1,128)}), s32[8,1,16]{2,1,0:T(1,128)S(1)}, u32[]{:S(2)}, u32[]{:S(2)}) async-start(s32[8,1,16]{2,1,0:T(1,128)} %bitcast.17), calls=%async_computation.2 | async-start | bytes 8192 | tf_op jit(solution)/shard_map/all_to_all | solution.py:145
  11.0 1.5 fusion.98
  12.5 1.8 multiply_reduce_fusion.4
  15.0 2.4 all-to-all-done.2
  17.4 3.6 %all-to-all-start = ((s32[8,1,16]{2,1,0:T(1,128)}), s32[8,1,16]{2,1,0:T(1,128)S(1)}, u32[]{:S(2)}, u32[]{:S(2)}) async-start(s32[8,1,16]{2,1,0:T(1,128)} %bitcast.8), calls=%async_computation | async-start | bytes 8192 | tf_op jit(solution)/shard_map/all_to_all | solution.py:146
  22.4 5.1 %all-to-all-done = s32[8,1,16]{2,1,0:T(1,128)S(1)} async-done(((s32[8,1,16]{2,1,0:T(1,128)}), s32[8,1,16]{2,1,0:T(1,128)S(1)}, u32[]{:S(2)}, u32[]{:S(2)}) %all-to-all-start) | async-done | bytes 544 | tf_op jit(solution)/shard_map/all_to_all | solution.py:146
  27.4 3.5 %all-to-all-start.1 = ((f32[8,16,4,256]{3,1,2,0:T(8,128)}), f32[8,16,4,256]{3,1,2,0:T(8,128)S(1)}, u32[]{:S(2)}, u32[]{:S(2)}) async-start(f32[8,16,4,256]{3,1,2,0:T(8,128)} %copy.111), calls=%async_computation.1 | async-start | bytes 1048576 | tf_op jit(solution)/shard_map/all_to_all | solution.py:144
  31.0 34.7 %all-reduce.3 = (f32[]{:T(128)}, f32[]{:T(128)}) all-reduce(f32[]{:T(128)} %get-tuple-element.64, f32[]{:T(128)} %get-tuple-element.62), channel_id=1, replica_groups=mesh['grp'=2,'gx'=4,'gy'=2,'gz'=2] {'gx','gy','gz'}, use_global_device_ids=true, to_apply=%region_1.0 | all-reduce | flops 2 | bytes 16 | tf_op jit(solution)/shard_map/psum | solution.py:124
  70.3 17.3 %while.10 = (s32[]{:T(128)}, f32[4,32,3,128]{3,2,1,0:T(4,128)S(1)}, bf16[4,32,3,256]{3,2,1,0:T(4,128)(2,1)S(1)}, s32[4,32]{1,0:T(4,128)S(1)}, bf16[32,256,128]{2,1,0:T(8,128)(2,1)S(1)}, /*index=5*/s32[]{:T(128)}) while((s32[]{:T(128)}, f32[4,32,3,128]{3,2,1,0:T(4,128)S(1)}, bf16[4,32,3,256]{3,2,1,0:T(4,128)(2,1)S(1)}, s32[4,32]{1,0:T(4,128)S(1)}, ...), condition=%wide.region_8.9_spmd, body=%wide.region_7.8_spmd.sunk | while | flops 7341346 | bytes 6428917 | solution.py:89
  70.4 2.2 gather_fusion
  72.6 2.1 fusion.120
  74.7 2.2 gather_fusion
  76.9 2.1 fusion.120
  79.0 2.2 gather_fusion
  81.2 2.1 fusion.120
  83.3 2.2 gather_fusion
  85.5 2.1 fusion.120
  88.9 3.5 %psum.65 = f32[3,32,128]{2,1,0:T(8,128)S(1)} all-reduce(f32[3,32,128]{2,1,0:T(8,128)S(1)} %reshape.93), channel_id=1, replica_groups=mesh['grp'=2,'gx'=4,'gy'=2,'gz'=2] {'gz'}, use_global_device_ids=true, to_apply=%region_9.10 | all-reduce | flops 12288 | bytes 98304 | tf_op jit(solution)/shard_map/psum | solution.py:162
  93.9 1.3 collective-permute-start.1
  95.4 4.2 %collective-permute-done.1 = f32[3,16,1,128]{3,1,2,0:T(8,128)S(1)} collective-permute-done((f32[3,16,1,128]{3,1,2,0:T(8,128)S(1)}, f32[3,16,1,128]{3,1,2,0:T(8,128)S(1)}, u32[]{:S(2)}, u32[]{:S(2)}) %collective-permute-start.1) | collective-permute-done | bytes 24608 | tf_op jit(solution)/shard_map/ppermute | solution.py:29
  104.0 3.9 %collective-permute-done.3 = f32[3,16,34,1]{2,1,3,0:T(8,128)S(1)} collective-permute-done((f32[3,16,34,1]{2,1,3,0:T(8,128)S(1)}, f32[3,16,34,1]{2,1,3,0:T(8,128)S(1)}, u32[]{:S(2)}, u32[]{:S(2)}) %collective-permute-start.3) | collective-permute-done | bytes 6560 | tf_op jit(solution)/shard_map/ppermute | solution.py:29
  109.1 1.3 collective-permute-start.4
  110.4 1.3 collective-permute-start.5
  111.7 1.9 collective-permute-done.5
  115.4 2.5 collective-permute-start.7
  117.9 1.3 collective-permute-start.6
  119.3 4.2 %collective-permute-done.6 = f32[16,1,128]{2,0,1:T(8,128)S(1)} collective-permute-done((f32[16,1,128]{2,0,1:T(8,128)S(1)}, f32[16,1,128]{2,0,1:T(8,128)S(1)}, u32[]{:S(2)}, u32[]{:S(2)}) %collective-permute-start.6) | collective-permute-done | bytes 8224 | tf_op jit(solution)/shard_map/ppermute | solution.py:29
  123.6 1.6 collective-permute-start.9
  125.3 1.3 collective-permute-start.8
  127.1 3.3 collective-permute-done.9
  130.3 4.1 %collective-permute-done.8 = f32[16,34,1]{2,0,1:T(8,128)S(1)} collective-permute-done((f32[16,34,1]{2,0,1:T(8,128)S(1)}, f32[16,34,1]{2,0,1:T(8,128)S(1)}, u32[]{:S(2)}, u32[]{:S(2)}) %collective-permute-start.8) | collective-permute-done | bytes 2208 | tf_op jit(solution)/shard_map/ppermute | solution.py:29
  134.8 1.3 collective-permute-start.10
  136.1 3.3 collective-permute-start.11
  141.7 30.5 %all-reduce.2 = (f32[]{:T(128)}, f32[]{:T(128)}) all-reduce(f32[]{:T(128)} %get-tuple-element.41, f32[]{:T(128)} %get-tuple-element.40), channel_id=1, replica_groups=mesh['grp'=2,'gx'=4,'gy'=2,'gz'=2] {'gx','gy','gz'}, use_global_device_ids=true, to_apply=%region_11.12 | all-reduce | flops 2 | bytes 16 | tf_op jit(solution)/shard_map/psum | solution.py:94
  175.0 1.3 collective-permute-start.13
  176.5 4.2 %collective-permute-done.13 = f32[3,16,1,128]{3,1,2,0:T(8,128)S(1)} collective-permute-done((f32[3,16,1,128]{3,1,2,0:T(8,128)S(1)}, f32[3,16,1,128]{3,1,2,0:T(8,128)S(1)}, u32[]{:S(2)}, u32[]{:S(2)}) %collective-permute-start.13) | collective-permute-done | bytes 24608 | tf_op jit(solution)/shard_map/ppermute | solution.py:29
  186.3 4.0 %collective-permute-done.15 = f32[3,16,34,1]{2,1,3,0:T(8,128)} collective-permute-done((f32[3,16,34,1]{2,1,3,0:T(8,128)S(1)}, f32[3,16,34,1]{2,1,3,0:T(8,128)}, u32[]{:S(2)}, u32[]{:S(2)}) %collective-permute-start.15) | collective-permute-done | bytes 6560 | tf_op jit(solution)/shard_map/ppermute | solution.py:29
  191.6 1.5 pad_maximum_fusion.75
  193.1 1.3 collective-permute-start.16
  194.4 1.3 collective-permute-start.17
  195.7 1.9 collective-permute-done.17
  199.4 2.0 collective-permute-start.19
  201.4 1.3 collective-permute-start.18
  202.7 4.2 %collective-permute-done.18 = f32[16,1,128]{2,0,1:T(8,128)S(1)} collective-permute-done((f32[16,1,128]{2,0,1:T(8,128)S(1)}, f32[16,1,128]{2,0,1:T(8,128)S(1)}, u32[]{:S(2)}, u32[]{:S(2)}) %collective-permute-start.18) | collective-permute-done | bytes 8224 | tf_op jit(solution)/shard_map/ppermute | solution.py:29
  207.1 1.5 collective-permute-start.21
  208.6 1.3 collective-permute-start.20
  210.4 3.1 collective-permute-done.21
  213.5 4.1 %collective-permute-done.20 = f32[16,34,1]{2,0,1:T(8,128)S(1)} collective-permute-done((f32[16,34,1]{2,0,1:T(8,128)S(1)}, f32[16,34,1]{2,0,1:T(8,128)S(1)}, u32[]{:S(2)}, u32[]{:S(2)}) %collective-permute-start.20) | collective-permute-done | bytes 2208 | tf_op jit(solution)/shard_map/ppermute | solution.py:29
  219.3 3.2 collective-permute-start.23
  225.0 30.5 %all-reduce.1 = (f32[]{:T(128)}, f32[]{:T(128)}) all-reduce(f32[]{:T(128)} %get-tuple-element.39, f32[]{:T(128)} %get-tuple-element.38), channel_id=1, replica_groups=mesh['grp'=2,'gx'=4,'gy'=2,'gz'=2] {'gx','gy','gz'}, use_global_device_ids=true, to_apply=%region_15.16 | all-reduce | flops 2 | bytes 16 | tf_op jit(solution)/shard_map/psum | solution.py:94
  263.0 4.2 %collective-permute-done.25 = f32[3,16,1,128]{3,1,2,0:T(8,128)S(1)} collective-permute-done((f32[3,16,1,128]{3,1,2,0:T(8,128)S(1)}, f32[3,16,1,128]{3,1,2,0:T(8,128)S(1)}, u32[]{:S(2)}, u32[]{:S(2)}) %collective-permute-start.25) | collective-permute-done | bytes 24608 | tf_op jit(solution)/shard_map/ppermute | solution.py:29
  268.5 1.6 copy.139
  271.8 1.5 collective-permute-start.27
  273.8 3.8 %collective-permute-done.27 = f32[3,16,34,1]{2,1,3,0:T(8,128)} collective-permute-done((f32[3,16,34,1]{2,1,3,0:T(8,128)S(1)}, f32[3,16,34,1]{2,1,3,0:T(8,128)}, u32[]{:S(2)}, u32[]{:S(2)}) %collective-permute-start.27) | collective-permute-done | bytes 6560 | tf_op jit(solution)/shard_map/ppermute | solution.py:29
  278.9 1.5 pad_maximum_fusion.70
  280.4 1.3 collective-permute-start.28
  283.0 1.9 collective-permute-done.29
  286.7 2.0 collective-permute-start.31
  290.0 4.2 %collective-permute-done.30 = f32[16,1,128]{2,0,1:T(8,128)S(1)} collective-permute-done((f32[16,1,128]{2,0,1:T(8,128)S(1)}, f32[16,1,128]{2,0,1:T(8,128)S(1)}, u32[]{:S(2)}, u32[]{:S(2)}) %collective-permute-start.30) | collective-permute-done | bytes 8224 | tf_op jit(solution)/shard_map/ppermute | solution.py:29
  294.4 1.5 collective-permute-start.33
  297.7 3.1 collective-permute-done.33
  300.8 4.1 %collective-permute-done.32 = f32[16,34,1]{2,0,1:T(8,128)S(1)} collective-permute-done((f32[16,34,1]{2,0,1:T(8,128)S(1)}, f32[16,34,1]{2,0,1:T(8,128)S(1)}, u32[]{:S(2)}, u32[]{:S(2)}) %collective-permute-start.32) | collective-permute-done | bytes 2208 | tf_op jit(solution)/shard_map/ppermute | solution.py:29
  306.6 3.2 collective-permute-start.35
  312.4 30.4 %all-reduce = (f32[]{:T(128)}, f32[]{:T(128)}) all-reduce(f32[]{:T(128)} %get-tuple-element.37, f32[]{:T(128)} %get-tuple-element.36), channel_id=1, replica_groups=mesh['grp'=2,'gx'=4,'gy'=2,'gz'=2] {'gx','gy','gz'}, use_global_device_ids=true, to_apply=%region_19.20 | all-reduce | flops 2 | bytes 16 | tf_op jit(solution)/shard_map/psum | solution.py:94
  (162 shorter events, 58.1 us)
Async XLA Ops:
  0.6 68.6 %copy-start = (f32[4,3]{1,0:T(4,128)S(1)}, f32[4,3]{1,0:T(4,128)}, u32[]{:S(2)}) copy-start(f32[4,3]{1,0:T(4,128)} %param.20) | copy-start | bytes 148
  0.6 66.3 %copy-start.17 = (f32[16]{0:T(128)S(1)}, f32[16]{0:T(128)}, u32[]{:S(2)}) copy-start(f32[16]{0:T(128)} %param.22) | copy-start | bytes 196
  3.7 13.7 %all-to-all-start.2 = ((s32[8,1,16]{2,1,0:T(1,128)}), s32[8,1,16]{2,1,0:T(1,128)S(1)}, u32[]{:S(2)}, u32[]{:S(2)}) async-start(s32[8,1,16]{2,1,0:T(1,128)} %bitcast.17), calls=%async_computation.2 | async-start | bytes 8192 | tf_op jit(solution)/shard_map/all_to_all | solution.py:145
  14.4 56.0 %copy-start.1 = (bf16[32,256,128]{2,1,0:T(8,128)(2,1)S(1)}, bf16[32,256,128]{2,1,0:T(8,128)(2,1)}, u32[]{:S(2)}) copy-start(bf16[32,256,128]{2,1,0:T(8,128)(2,1)} %param.21) | copy-start | bytes 6291460
  17.4 10.1 %all-to-all-start = ((s32[8,1,16]{2,1,0:T(1,128)}), s32[8,1,16]{2,1,0:T(1,128)S(1)}, u32[]{:S(2)}, u32[]{:S(2)}) async-start(s32[8,1,16]{2,1,0:T(1,128)} %bitcast.8), calls=%async_computation | async-start | bytes 8192 | tf_op jit(solution)/shard_map/all_to_all | solution.py:146
  27.4 41.5 %all-to-all-start.1 = ((f32[8,16,4,256]{3,1,2,0:T(8,128)}), f32[8,16,4,256]{3,1,2,0:T(8,128)S(1)}, u32[]{:S(2)}, u32[]{:S(2)}) async-start(f32[8,16,4,256]{3,1,2,0:T(8,128)} %copy.111), calls=%async_computation.1 | async-start | bytes 1048576 | tf_op jit(solution)/shard_map/all_to_all | solution.py:144
  92.4 7.5 %copy-start.9 = (f32[3,32,128]{2,1,0:T(8,128)}, f32[3,32,128]{2,1,0:T(8,128)S(1)}, u32[]{:S(2)}) copy-start(f32[3,32,128]{2,1,0:T(8,128)S(1)} %psum.65) | copy-start | bytes 147460
  92.6 2.8 collective-permute-start
  93.9 5.7 %collective-permute-start.1 = (f32[3,16,1,128]{3,1,2,0:T(8,128)S(1)}, f32[3,16,1,128]{3,1,2,0:T(8,128)S(1)}, u32[]{:S(2)}, u32[]{:S(2)}) collective-permute-start(f32[3,16,1,128]{3,1,2,0:T(8,128)S(1)} %get-tuple-element.100), channel_id=1, source_target_pairs={{4,0},{8,4},{12,8},{5,1},{9,5},{13,9},{6,2},{10,6},{14,10},{7,3},{... | collective-permute-start | bytes 73736 | tf_op jit(solution)/shard_map/ppermute | solution.py:29
  100.4 3.1 collective-permute-start.2
  102.2 5.7 %collective-permute-start.3 = (f32[3,16,34,1]{2,1,3,0:T(8,128)S(1)}, f32[3,16,34,1]{2,1,3,0:T(8,128)S(1)}, u32[]{:S(2)}, u32[]{:S(2)}) collective-permute-start(f32[3,16,34,1]{2,1,3,0:T(8,128)S(1)} %copy.136), channel_id=1, source_target_pairs={{2,0},{3,1},{6,4},{7,5},{10,8},{11,9},{14,12},{15,13},{18,16},{19,... | collective-permute-start | bytes 19592 | tf_op jit(solution)/shard_map/ppermute | solution.py:29
  109.1 2.6 collective-permute-start.4
  110.4 3.2 collective-permute-start.5
  115.0 11.6 %copy-start.2 = (f32[16,32,128]{2,1,0:T(8,128)S(1)}, f32[16,32,128]{2,1,0:T(8,128)}, u32[]{:S(2)}) copy-start(f32[16,32,128]{2,1,0:T(8,128)} %param.23) | copy-start | bytes 786436
  115.4 3.8 %collective-permute-start.7 = (f32[16,1,128]{2,0,1:T(8,128)S(1)}, f32[16,1,128]{2,0,1:T(8,128)S(1)}, u32[]{:S(2)}, u32[]{:S(2)}) collective-permute-start(f32[16,1,128]{2,0,1:T(8,128)S(1)} %get-tuple-element.111), channel_id=1, source_target_pairs={{0,4},{4,8},{8,12},{1,5},{5,9},{9,13},{2,6},{6,10},{10,14},{3,7},{... | collective-permute-start | bytes 24584 | tf_op jit(solution)/shard_map/ppermute | solution.py:27
  117.9 5.5 %collective-permute-start.6 = (f32[16,1,128]{2,0,1:T(8,128)S(1)}, f32[16,1,128]{2,0,1:T(8,128)S(1)}, u32[]{:S(2)}, u32[]{:S(2)}) collective-permute-start(f32[16,1,128]{2,0,1:T(8,128)S(1)} %get-tuple-element.112), channel_id=1, source_target_pairs={{4,0},{8,4},{12,8},{5,1},{9,5},{13,9},{6,2},{10,6},{14,10},{7,3},{... | collective-permute-start | bytes 24584 | tf_op jit(solution)/shard_map/ppermute | solution.py:29
  123.6 6.7 %collective-permute-start.9 = (f32[16,34,1]{2,0,1:T(8,128)S(1)}, f32[16,34,1]{2,0,1:T(8,128)S(1)}, u32[]{:S(2)}, u32[]{:S(2)}) collective-permute-start(f32[16,34,1]{2,0,1:T(8,128)S(1)} %get-tuple-element.105), channel_id=1, source_target_pairs={{0,2},{1,3},{4,6},{5,7},{8,10},{9,11},{12,14},{13,15},{16,18},{17,... | collective-permute-start | bytes 6536 | tf_op jit(solution)/shard_map/ppermute | solution.py:27
  125.3 9.2 %collective-permute-start.8 = (f32[16,34,1]{2,0,1:T(8,128)S(1)}, f32[16,34,1]{2,0,1:T(8,128)S(1)}, u32[]{:S(2)}, u32[]{:S(2)}) collective-permute-start(f32[16,34,1]{2,0,1:T(8,128)S(1)} %get-tuple-element.106), channel_id=1, source_target_pairs={{2,0},{3,1},{6,4},{7,5},{10,8},{11,9},{14,12},{15,13},{18,16},{19,... | collective-permute-start | bytes 6536 | tf_op jit(solution)/shard_map/ppermute | solution.py:29
  134.8 5.3 %collective-permute-start.10 = (f32[1,34,130]{2,0,1:T(1,128)S(1)}, f32[1,34,130]{2,0,1:T(1,128)S(1)}, u32[]{:S(2)}, u32[]{:S(2)}) collective-permute-start(f32[1,34,130]{2,0,1:T(1,128)S(1)} %get-tuple-element.89), channel_id=1, source_target_pairs={{1,0},{3,2},{5,4},{7,6},{9,8},{11,10},{13,12},{15,14},{17,16},{19,... | collective-permute-start | bytes 53048 | tf_op jit(solution)/shard_map/ppermute | solution.py:29
  136.1 4.7 %copy-start.10 = (f32[3,32,128]{2,1,0:T(8,128)S(1)}, f32[3,32,128]{2,1,0:T(8,128)}, u32[]{:S(2)}) copy-start(f32[3,32,128]{2,1,0:T(8,128)} %copy-done.9) | copy-start | bytes 147460
  136.1 4.0 %collective-permute-start.11 = (f32[1,34,130]{2,0,1:T(1,128)S(1)}, f32[1,34,130]{2,0,1:T(1,128)S(1)}, u32[]{:S(2)}, u32[]{:S(2)}) collective-permute-start(f32[1,34,130]{2,0,1:T(1,128)S(1)} %get-tuple-element.90), channel_id=1, source_target_pairs={{0,1},{2,3},{4,5},{6,7},{8,9},{10,11},{12,13},{14,15},{16,17},{18,... | collective-permute-start | bytes 53048 | tf_op jit(solution)/shard_map/ppermute | solution.py:27
  173.7 2.8 collective-permute-start.12
  175.0 5.7 %collective-permute-start.13 = (f32[3,16,1,128]{3,1,2,0:T(8,128)S(1)}, f32[3,16,1,128]{3,1,2,0:T(8,128)S(1)}, u32[]{:S(2)}, u32[]{:S(2)}) collective-permute-start(f32[3,16,1,128]{3,1,2,0:T(8,128)S(1)} %get-tuple-element.98), channel_id=1, source_target_pairs={{4,0},{8,4},{12,8},{5,1},{9,5},{13,9},{6,2},{10,6},{14,10},{7,3},{... | collective-permute-start | bytes 73736 | tf_op jit(solution)/shard_map/ppermute | solution.py:29
  180.7 0.6 copy-start.13
  182.8 3.0 collective-permute-start.14
  184.5 5.8 %collective-permute-start.15 = (f32[3,16,34,1]{2,1,3,0:T(8,128)S(1)}, f32[3,16,34,1]{2,1,3,0:T(8,128)}, u32[]{:S(2)}, u32[]{:S(2)}) collective-permute-start(f32[3,16,34,1]{2,1,3,0:T(8,128)S(1)} %copy.138), channel_id=1, source_target_pairs={{2,0},{3,1},{6,4},{7,5},{10,8},{11,9},{14,12},{15,13},{18,16},{19,... | collective-permute-start | bytes 19592 | tf_op jit(solution)/shard_map/ppermute | solution.py:29
  191.6 6.0 %copy-start.14 = (f32[3,16,1,128]{3,1,2,0:T(8,128)S(1)}, f32[3,16,1,128]{3,1,2,0:T(8,128)}, u32[]{:S(2)}) copy-start(f32[3,16,1,128]{3,1,2,0:T(8,128)} %copy-done.13) | copy-start | bytes 73732
  193.1 2.6 collective-permute-start.16
  194.4 3.2 collective-permute-start.17
  199.4 3.3 collective-permute-start.19
  201.4 5.5 %collective-permute-start.18 = (f32[16,1,128]{2,0,1:T(8,128)S(1)}, f32[16,1,128]{2,0,1:T(8,128)S(1)}, u32[]{:S(2)}, u32[]{:S(2)}) collective-permute-start(f32[16,1,128]{2,0,1:T(8,128)S(1)} %get-tuple-element.110), channel_id=1, source_target_pairs={{4,0},{8,4},{12,8},{5,1},{9,5},{13,9},{6,2},{10,6},{14,10},{7,3},{... | collective-permute-start | bytes 24584 | tf_op jit(solution)/shard_map/ppermute | solution.py:29
  207.1 6.5 %collective-permute-start.21 = (f32[16,34,1]{2,0,1:T(8,128)S(1)}, f32[16,34,1]{2,0,1:T(8,128)S(1)}, u32[]{:S(2)}, u32[]{:S(2)}) collective-permute-start(f32[16,34,1]{2,0,1:T(8,128)S(1)} %get-tuple-element.103), channel_id=1, source_target_pairs={{0,2},{1,3},{4,6},{5,7},{8,10},{9,11},{12,14},{13,15},{16,18},{17,... | collective-permute-start | bytes 6536 | tf_op jit(solution)/shard_map/ppermute | solution.py:27
  208.6 9.0 %collective-permute-start.20 = (f32[16,34,1]{2,0,1:T(8,128)S(1)}, f32[16,34,1]{2,0,1:T(8,128)S(1)}, u32[]{:S(2)}, u32[]{:S(2)}) collective-permute-start(f32[16,34,1]{2,0,1:T(8,128)S(1)} %get-tuple-element.104), channel_id=1, source_target_pairs={{2,0},{3,1},{6,4},{7,5},{10,8},{11,9},{14,12},{15,13},{18,16},{19,... | collective-permute-start | bytes 6536 | tf_op jit(solution)/shard_map/ppermute | solution.py:29
  210.4 49.5 %copy-start.3 = (f32[1,16,32,128]{3,1,2,0:T(8,128)}, f32[1,16,32,128]{3,1,2,0:T(8,128)S(1)}, u32[]{:S(2)}) copy-start(f32[1,16,32,128]{3,1,2,0:T(8,128)S(1)} %fusion.59) | copy-start | bytes 786436
  218.0 5.1 %collective-permute-start.22 = (f32[1,34,130]{2,0,1:T(1,128)S(1)}, f32[1,34,130]{2,0,1:T(1,128)S(1)}, u32[]{:S(2)}, u32[]{:S(2)}) collective-permute-start(f32[1,34,130]{2,0,1:T(1,128)S(1)} %get-tuple-element.85), channel_id=1, source_target_pairs={{1,0},{3,2},{5,4},{7,6},{9,8},{11,10},{13,12},{15,14},{17,16},{19,... | collective-permute-start | bytes 53048 | tf_op jit(solution)/shard_map/ppermute | solution.py:29
  219.3 4.7 %copy-start.11 = (f32[3,32,128]{2,1,0:T(8,128)S(1)}, f32[3,32,128]{2,1,0:T(8,128)}, u32[]{:S(2)}) copy-start(f32[3,32,128]{2,1,0:T(8,128)} %copy-done.9) | copy-start | bytes 147460
  219.3 4.0 %collective-permute-start.23 = (f32[1,34,130]{2,0,1:T(1,128)S(1)}, f32[1,34,130]{2,0,1:T(1,128)S(1)}, u32[]{:S(2)}, u32[]{:S(2)}) collective-permute-start(f32[1,34,130]{2,0,1:T(1,128)S(1)} %get-tuple-element.86), channel_id=1, source_target_pairs={{0,1},{2,3},{4,5},{6,7},{8,9},{10,11},{12,13},{14,15},{16,17},{18,... | collective-permute-start | bytes 53048 | tf_op jit(solution)/shard_map/ppermute | solution.py:27
  223.1 37.0 %copy-start.5 = (f32[1,16,32,128]{3,1,2,0:T(8,128)}, f32[1,16,32,128]{3,1,2,0:T(8,128)S(1)}, u32[]{:S(2)}) copy-start(f32[1,16,32,128]{3,1,2,0:T(8,128)S(1)} %fusion.51) | copy-start | bytes 786436
  224.0 43.3 %copy-start.7 = (f32[1,16,32,128]{3,1,2,0:T(8,128)}, f32[1,16,32,128]{3,1,2,0:T(8,128)S(1)}, u32[]{:S(2)}) copy-start(f32[1,16,32,128]{3,1,2,0:T(8,128)S(1)} %fusion.45) | copy-start | bytes 786436
  260.2 2.8 collective-permute-start.24
  261.5 5.7 %collective-permute-start.25 = (f32[3,16,1,128]{3,1,2,0:T(8,128)S(1)}, f32[3,16,1,128]{3,1,2,0:T(8,128)S(1)}, u32[]{:S(2)}, u32[]{:S(2)}) collective-permute-start(f32[3,16,1,128]{3,1,2,0:T(8,128)S(1)} %get-tuple-element.96), channel_id=1, source_target_pairs={{4,0},{8,4},{12,8},{5,1},{9,5},{13,9},{6,2},{10,6},{14,10},{7,3},{... | collective-permute-start | bytes 73736 | tf_op jit(solution)/shard_map/ppermute | solution.py:29
  267.2 1.3 copy-start.15
  270.0 3.3 collective-permute-start.26
  271.8 5.8 %collective-permute-start.27 = (f32[3,16,34,1]{2,1,3,0:T(8,128)S(1)}, f32[3,16,34,1]{2,1,3,0:T(8,128)}, u32[]{:S(2)}, u32[]{:S(2)}) collective-permute-start(f32[3,16,34,1]{2,1,3,0:T(8,128)S(1)} %copy.140), channel_id=1, source_target_pairs={{2,0},{3,1},{6,4},{7,5},{10,8},{11,9},{14,12},{15,13},{18,16},{19,... | collective-permute-start | bytes 19592 | tf_op jit(solution)/shard_map/ppermute | solution.py:29
  278.9 6.0 %copy-start.16 = (f32[3,16,1,128]{3,1,2,0:T(8,128)S(1)}, f32[3,16,1,128]{3,1,2,0:T(8,128)}, u32[]{:S(2)}) copy-start(f32[3,16,1,128]{3,1,2,0:T(8,128)} %copy-done.15) | copy-start | bytes 73732
  280.4 2.6 collective-permute-start.28
  281.7 3.2 collective-permute-start.29
  286.7 3.3 collective-permute-start.31
  288.7 5.5 %collective-permute-start.30 = (f32[16,1,128]{2,0,1:T(8,128)S(1)}, f32[16,1,128]{2,0,1:T(8,128)S(1)}, u32[]{:S(2)}, u32[]{:S(2)}) collective-permute-start(f32[16,1,128]{2,0,1:T(8,128)S(1)} %get-tuple-element.108), channel_id=1, source_target_pairs={{4,0},{8,4},{12,8},{5,1},{9,5},{13,9},{6,2},{10,6},{14,10},{7,3},{... | collective-permute-start | bytes 24584 | tf_op jit(solution)/shard_map/ppermute | solution.py:29
  294.4 6.4 %collective-permute-start.33 = (f32[16,34,1]{2,0,1:T(8,128)S(1)}, f32[16,34,1]{2,0,1:T(8,128)S(1)}, u32[]{:S(2)}, u32[]{:S(2)}) collective-permute-start(f32[16,34,1]{2,0,1:T(8,128)S(1)} %get-tuple-element.101), channel_id=1, source_target_pairs={{0,2},{1,3},{4,6},{5,7},{8,10},{9,11},{12,14},{13,15},{16,18},{17,... | collective-permute-start | bytes 6536 | tf_op jit(solution)/shard_map/ppermute | solution.py:27
  295.9 9.0 %collective-permute-start.32 = (f32[16,34,1]{2,0,1:T(8,128)S(1)}, f32[16,34,1]{2,0,1:T(8,128)S(1)}, u32[]{:S(2)}, u32[]{:S(2)}) collective-permute-start(f32[16,34,1]{2,0,1:T(8,128)S(1)} %get-tuple-element.102), channel_id=1, source_target_pairs={{2,0},{3,1},{6,4},{7,5},{10,8},{11,9},{14,12},{15,13},{18,16},{19,... | collective-permute-start | bytes 6536 | tf_op jit(solution)/shard_map/ppermute | solution.py:29
  305.2 5.2 %collective-permute-start.34 = (f32[1,34,130]{2,0,1:T(1,128)S(1)}, f32[1,34,130]{2,0,1:T(1,128)S(1)}, u32[]{:S(2)}, u32[]{:S(2)}) collective-permute-start(f32[1,34,130]{2,0,1:T(1,128)S(1)} %get-tuple-element.81), channel_id=1, source_target_pairs={{1,0},{3,2},{5,4},{7,6},{9,8},{11,10},{13,12},{15,14},{17,16},{19,... | collective-permute-start | bytes 53048 | tf_op jit(solution)/shard_map/ppermute | solution.py:29
  306.5 4.7 %copy-start.4 = (f32[1,16,32,128]{3,1,2,0:T(8,128)S(1)}, f32[1,16,32,128]{3,1,2,0:T(8,128)}, u32[]{:S(2)}) copy-start(f32[1,16,32,128]{3,1,2,0:T(8,128)} %copy-done.3) | copy-start | bytes 786436
  306.5 4.7 %copy-start.6 = (f32[1,16,32,128]{3,1,2,0:T(8,128)S(1)}, f32[1,16,32,128]{3,1,2,0:T(8,128)}, u32[]{:S(2)}) copy-start(f32[1,16,32,128]{3,1,2,0:T(8,128)} %copy-done.5) | copy-start | bytes 786436
  306.5 4.7 %copy-start.8 = (f32[1,16,32,128]{3,1,2,0:T(8,128)S(1)}, f32[1,16,32,128]{3,1,2,0:T(8,128)}, u32[]{:S(2)}) copy-start(f32[1,16,32,128]{3,1,2,0:T(8,128)} %copy-done.7) | copy-start | bytes 786436
  306.6 4.7 %copy-start.12 = (f32[3,32,128]{2,1,0:T(8,128)S(1)}, f32[3,32,128]{2,1,0:T(8,128)}, u32[]{:S(2)}) copy-start(f32[3,32,128]{2,1,0:T(8,128)} %copy-done.9) | copy-start | bytes 147460
  306.6 4.0 %collective-permute-start.35 = (f32[1,34,130]{2,0,1:T(1,128)S(1)}, f32[1,34,130]{2,0,1:T(1,128)S(1)}, u32[]{:S(2)}, u32[]{:S(2)}) collective-permute-start(f32[1,34,130]{2,0,1:T(1,128)S(1)} %get-tuple-element.82), channel_id=1, source_target_pairs={{0,1},{2,3},{4,5},{6,7},{8,9},{10,11},{12,13},{14,15},{16,17},{18,... | collective-permute-start | bytes 53048 | tf_op jit(solution)/shard_map/ppermute | solution.py:27
where the time goes:
time: 351 us; the launch traced here: 349 us
  blocking collectives  130 us (37%)
  waiting for transfers between devices  73.2 us (21%)
  starting transfers between devices  70.3 us (20%)
  local copies, waits for them, and re-layouts  26.9 us (8%)
  other arithmetic  26.2 us (7%)
  between operations  12.4 us (4%)
  matrix products  10.8 us (3%)
    psum x3, blocking collectives, two_products(): lax.psum((jnp.sum(residual * residual), jnp.sum(residual * image)), ('gx'...  91.4 us
    ppermute x18, waiting for transfers between devices, extended(): lax.ppermute(head, axis, [((i + 1) % count, i) for i in range(ends)])  55 us
    psum x1, blocking collectives, per_device(): lax.psum((jnp.sum(resid * resid), jnp.sum(valid)), ('gx', 'gy', 'gz'))  34.7 us
    ppermute x18, starting transfers between devices, extended(): lax.ppermute(tail, axis, [(i, (i + 1) % count) for i in range(ends)])  32.4 us
    ppermute x18, starting transfers between devices, extended(): lax.ppermute(head, axis, [((i + 1) % count, i) for i in range(ends)])  23.5 us
    ppermute x18, waiting for transfers between devices, extended(): lax.ppermute(tail, axis, [(i, (i + 1) % count) for i in range(ends)])  10.7 us
    gather x4, local copies, waits for them, and re-layouts, per_group(): selected_entries = jnp.take(weights, block_tables, axis=0)  8.72 us
    dot_general x4, matrix products, per_group(): jnp.einsum('aow,awv->aov', block_coefficient_values, selected_entries, pr...  8.3 us
  transfers between devices with their start and end apart: 39, of which 25 were waited for; matrix products, arithmetic and copies ran while one was open for 4% of the time, Pallas kernels for 0%

commit v1 on v0

v1 whole, which is shorter than its diff:
```python
import functools

import jax
import jax.numpy as jnp
from jax import lax
from jax.experimental import pallas as pl
from jax.experimental.pallas import tpu as pltpu
from jax.sharding import PartitionSpec as P

PATCH_X = 8
PATCH_Y = 16
ITERS = 3
KAPPA = 0.5
EPS = 1e-06
SHIFT = 8.0
HX = 8
LANES = 128
MESH = pl.DeviceIdType.MESH
F32 = jnp.float32
BF16 = jnp.bfloat16


def split_dot(one_hot, values):
    high = values.astype(BF16)
    low = (values - high.astype(F32)).astype(BF16)
    return jnp.dot(one_hot, high, preferred_element_type=F32) + jnp.dot(
        one_hot, low, preferred_element_type=F32
    )


def dot_split(values, one_hot):
    high = values.astype(BF16)
    low = (values - high.astype(F32)).astype(BF16)
    return jnp.dot(high, one_hot, preferred_element_type=F32) + jnp.dot(
        low, one_hot, preferred_element_type=F32
    )


def up(a, axis):
    return pltpu.roll(a, a.shape[axis] - 1, axis)


def down(a, axis):
    return pltpu.roll(a, 1, axis)


def lane_roll(a, amount):
    amount = amount % LANES
    return a if amount == 0 else pltpu.roll(a, amount, a.ndim - 1)


def body(
    ngx, ngy, ngz, cap, epochs,
    choice, depth, partial, owner_ref, patch_ref, coeffs, weights, stiff,
    v1_out, v2_out, v3_out, surf_out, coef_out,
    sums, send, meta, recv, metarecv, part, ppk, msum, sx, sy, sc, mz,
    dext, kext, pk, pkrecv, surf, v1, v2, v3, div, fields, momsend, mom,
    a_send, a_recv, m_send, m_recv, kx_sem, ky_sem, kz_sem, dz_sem,
    h_send, sx_sem, sy_sem, sc_sem, mz_sem, r_send, r_recv, out_sem,
):
    gx = lax.axis_index("gx")
    gy = lax.axis_index("gy")
    gz = lax.axis_index("gz")
    owners = ngx * ngy
    total = owners * ngz
    me = gx * ngy + gy
    flat = me * ngz + gz
    nz, lx, ly = stiff.shape
    blocks = choice.shape[0]
    rows_x = lx + 2 * HX
    width = 2 * LANES
    places_x = lx // PATCH_X
    places_y = ly // PATCH_Y
    places = places_x * places_y
    cells = PATCH_X * PATCH_Y
    slots = owners * cap
    meta_w = meta.shape[2]

    def at(x, y, z):
        return {"gx": x, "gy": y, "gz": z}

    def peer_of(t):
        p = lax.rem(flat + t, total)
        q = p // ngz
        return p, at(q // ngy, lax.rem(q, ngy), lax.rem(p, ngz))

    barrier = pltpu.get_barrier_semaphore()

    def greet(t, carry):
        _, device = peer_of(t)
        pl.semaphore_signal(barrier, inc=1, device_id=device, device_id_type=MESH)
        return carry

    lax.fori_loop(1, total, greet, 0)

    def copy(src, dst, send_sem, recv_sem, device):
        return pltpu.make_async_remote_copy(
            src_ref=src, dst_ref=dst, send_sem=send_sem, recv_sem=recv_sem,
            device_id=device, device_id_type=MESH,
        )

    for b in range(blocks):
        table = weights[choice[b]]
        sums[b] = jnp.dot(coeffs[b], table, preferred_element_type=F32)

    for z in range(nz):
        dext[z + 6] = jnp.full((8, LANES), depth[z], F32)
    kext[4:4 + nz, HX:HX + lx, 0:LANES] = stiff[...]

    owner_col = owner_ref[...]
    patch_col = patch_ref[...]
    rows_i = lax.broadcasted_iota(jnp.int32, (blocks, blocks), 0)
    cols_i = lax.broadcasted_iota(jnp.int32, (blocks, blocks), 1)
    owner_wide = jnp.broadcast_to(owner_col, (blocks, blocks))
    owner_row = jnp.sum(jnp.where(rows_i == cols_i, owner_wide, 0), axis=0, keepdims=True)
    same = owner_wide == owner_row
    rank_row = jnp.sum(jnp.where(same & (rows_i < cols_i), 1, 0), axis=0, keepdims=True)
    rank_col = jnp.sum(jnp.where(same & (cols_i < rows_i), 1, 0), axis=1, keepdims=True)
    slot_row = owner_row * cap + rank_row
    slot_ids = lax.broadcasted_iota(jnp.int32, (slots, blocks), 0)
    select = jnp.where(slot_ids == slot_row, 1.0, 0.0).astype(BF16)
    for c in range(3):
        sent = split_dot(select, sums[:, c, :])
        send[:, c * cap:(c + 1) * cap, :] = sent.reshape(owners, cap, cells)
    lane_ids = lax.broadcasted_iota(jnp.int32, (blocks, meta_w), 1)
    ranked = jnp.where(lane_ids == rank_col + me * cap, patch_col, 0).astype(F32).astype(BF16)
    owner_ids = lax.broadcasted_iota(jnp.int32, (max(8, owners), blocks), 0)
    owner_hot = jnp.where(owner_ids == owner_row, 1.0, 0.0).astype(BF16)
    patches = jnp.dot(owner_hot, ranked, preferred_element_type=F32)
    sub_ids = lax.broadcasted_iota(jnp.int32, (8, meta_w), 0)
    extras = jnp.where(sub_ids == 1, partial[0], jnp.where(sub_ids == 2, partial[1], 0.0))
    for o in range(owners):
        line = jnp.broadcast_to(patches[o:o + 1, :], (8, meta_w))
        meta[o] = jnp.where(sub_ids == 0, line, extras)

    pl.semaphore_wait(barrier, total - 1)

    exchange = []
    for t in range(1, owners):
        o = lax.rem(me + t, owners)
        src = lax.rem(me + owners - t, owners)
        device = at(o // ngy, lax.rem(o, ngy), gz)
        data = copy(send.at[o], recv.at[me], a_send.at[t], a_recv.at[me], device)
        note = copy(meta.at[o], metarecv.at[me], m_send.at[t], m_recv.at[me], device)
        data.start()
        note.start()
        exchange.append((
            data, note,
            copy(send.at[o], recv.at[src], a_send.at[t], a_recv.at[src], device),
            copy(meta.at[o], metarecv.at[src], m_send.at[t], m_recv.at[src], device),
        ))

    def both_sides(position, count, axis, low_src, low_dst, high_src, high_dst, sem, fill):
        others = {"gx": gx, "gy": gy, "gz": gz}
        lower, upper = dict(others), dict(others)
        lower[axis] = position - 1
        upper[axis] = position + 1
        to_low = copy(low_src, high_dst, sem.at[0], sem.at[1], lower)
        to_high = copy(high_src, low_dst, sem.at[2], sem.at[3], upper)
        has_low = position > 0
        has_high = position < count - 1
        pl.when(has_low)(lambda: to_low.start())
        pl.when(has_high)(lambda: to_high.start())
        pl.when(jnp.logical_not(has_low))(lambda: fill(low_dst))
        pl.when(jnp.logical_not(has_high))(lambda: fill(high_dst))

        def finish():
            @pl.when(has_low)
            def _():
                to_low.wait_send()
                copy(low_src, low_dst, sem.at[2], sem.at[3], lower).wait_recv()

            @pl.when(has_high)
            def _():
                to_high.wait_send()
                copy(high_src, high_dst, sem.at[0], sem.at[1], upper).wait_recv()

        return finish

    def zero(ref):
        ref[...] = jnp.zeros(ref.shape, F32)

    finish_x = both_sides(
        gx, ngx, "gx",
        stiff.at[:, pl.ds(0, HX), :],
        kext.at[pl.ds(4, nz), pl.ds(0, HX), pl.ds(0, LANES)],
        stiff.at[:, pl.ds(lx - HX, HX), :],
        kext.at[pl.ds(4, nz), pl.ds(HX + lx, HX), pl.ds(0, LANES)],
        kx_sem, zero,
    )
    finish_d = both_sides(
        gz, ngz, "gz",
        dext.at[pl.ds(6, 6)], dext.at[pl.ds(0, 6)],
        dext.at[pl.ds(nz, 6)], dext.at[pl.ds(nz + 6, 6)],
        dz_sem, zero,
    )
    finish_x()
    lane1 = lax.broadcasted_iota(jnp.int32, (rows_x, LANES), 1)
    for g in range(nz // 8):
        left = jnp.zeros((rows_x, LANES), F32)
        right = jnp.zeros((rows_x, LANES), F32)
        for k in range(8):
            plane = kext[4 + 8 * g + k, :, 0:LANES]
            here = (lane1 // 16) == k
            left = jnp.where(here, lane_roll(plane, 16 * k), left)
            right = jnp.where(here, lane_roll(plane, 16 * k + 16), right)
        pk[0, g] = left
        pk[1, g] = right
    finish_y = both_sides(
        gy, ngy, "gy", pk.at[0], pkrecv.at[0], pk.at[1], pkrecv.at[1], ky_sem, zero
    )
    finish_y()
    for g in range(nz // 8):
        from_left = pkrecv[0, g]
        from_right = pkrecv[1, g]
        for k in range(8):
            kext[4 + 8 * g + k, :, LANES:width] = jnp.where(
                lane1 < 64, lane_roll(from_right, -16 * k), lane_roll(from_left, 112 - 16 * k)
            )
    finish_z = both_sides(
        gz, ngz, "gz",
        kext.at[pl.ds(4, 4)], kext.at[pl.ds(0, 4)],
        kext.at[pl.ds(nz, 4)], kext.at[pl.ds(nz + 4, 4)],
        kz_sem, zero,
    )

    recv[me] = send[me]
    metarecv[me] = meta[me]
    for data, note, data_in, note_in in exchange:
        data_in.wait_recv()
        note_in.wait_recv()

    notes = metarecv[0]
    for s in range(1, owners):
        notes = notes + metarecv[s]
    patch_row = notes[0:1, 0:slots]
    place_ids = lax.broadcasted_iota(jnp.int32, (places, slots), 0).astype(F32)
    place_hot = jnp.where(place_ids == patch_row, 1.0, 0.0).astype(BF16)
    msum[...] = notes[:, 0:LANES]
    cell_i = lax.broadcasted_iota(jnp.int32, (cells, PATCH_X * LANES), 0)
    lane_i = lax.broadcasted_iota(jnp.int32, (cells, PATCH_X * LANES), 1)
    spread = jnp.where(
        cell_i == (lane_i // LANES) * PATCH_Y + lane_i % PATCH_Y, 1.0, 0.0
    ).astype(BF16)
    wide_lane = lax.broadcasted_iota(jnp.int32, (places, PATCH_X * LANES), 1)
    wide_row = lax.broadcasted_iota(jnp.int32, (places, PATCH_X * LANES), 0)
    own_place = (wide_lane % LANES) // PATCH_Y == wide_row % places_y
    for c in range(3):
        arrived = recv[:, c * cap:(c + 1) * cap, :].reshape(slots, cells)
        placed = split_dot(place_hot, arrived)
        expanded = jnp.where(own_place, dot_split(placed, spread), 0.0)
        lines = jnp.sum(expanded.reshape(places_x, places_y, PATCH_X * LANES), axis=1)
        for i in range(PATCH_X):
            for px in range(places_x):
                row = px * PATCH_X + i
                part[c, row:row + 1, :] = lines[px:px + 1, i * LANES:(i + 1) * LANES]

    lane8 = lax.broadcasted_iota(jnp.int32, (8, LANES), 1)
    groups = lx // 8
    packs = ppk.shape[1]
    left = [jnp.zeros((8, LANES), F32)] * packs
    right = [jnp.zeros((8, LANES), F32)] * packs
    for c in range(3):
        for r in range(groups):
            k = c * groups + r
            q, kk = k // 8, k % 8
            tile = part[c, r * 8:(r + 1) * 8, :]
            here = (lane8 // 16) == kk
            left[q] = jnp.where(here, lane_roll(tile, 16 * kk), left[q])
            right[q] = jnp.where(here, lane_roll(tile, 16 * kk + 16), right[q])
    for q in range(packs):
        ppk[0, q] = left[q]
        ppk[1, q] = right[q]

    sends, receives = [], []
    number = 0
    for t in range(1, ngz):
        z = lax.rem(gz + t, ngz)
        for src, dst, sem in ((part, sc, sc_sem), (msum, mz, mz_sem)):
            out = copy(src, dst.at[gz], h_send.at[number], sem.at[gz], at(gx, gy, z))
            out.start()
            sends.append((None, out))
            receives.append((None, copy(src, dst.at[z], h_send.at[number], sem.at[z], at(gx, gy, z))))
            number += 1
    for dx in (-1, 0, 1):
        for dy in (-1, 0, 1):
            if dx == 0 and dy == 0:
                continue
            nx, ny = gx + dx, gy + dy
            there = (nx >= 0) & (nx < ngx) & (ny >= 0) & (ny < ngy)
            for z in range(ngz):
                device = at(nx, ny, z)
                if dy == 0:
                    src = part.at[:, pl.ds(lx - 8 if dx > 0 else 0, 8), :]
                    side_out, side_in = (0, 1) if dx > 0 else (1, 0)
                    out = copy(src, sx.at[side_out, gz], h_send.at[number],
                               sx_sem.at[side_out, gz], device)
                    came = copy(src, sx.at[side_in, z], h_send.at[number],
                                sx_sem.at[side_in, z], device)
                    hole = sx.at[side_in, z]
                else:
                    src = ppk.at[1 if dy > 0 else 0]
                    side_out, side_in = (0, 1) if dy > 0 else (1, 0)
                    out = copy(src, sy.at[1 - dx, side_out, gz], h_send.at[number],
                               sy_sem.at[1 - dx, side_out, gz], device)
                    came = copy(src, sy.at[1 + dx, side_in, z], h_send.at[number],
                                sy_sem.at[1 + dx, side_in, z], device)
                    hole = sy.at[1 + dx, side_in, z]
                pl.when(there)(lambda out=out: out.start())
                pl.when(jnp.logical_not(there))(lambda hole=hole: zero(hole))
                sends.append((there, out))
                receives.append((there, came))
                number += 1
    sc[gz] = part[...]
    mz[gz] = msum[...]
    finish_d()
    finish_z()
    for there, came in receives:
        if there is None:
            came.wait_recv()
        else:
            pl.when(there)(lambda came=came: came.wait_recv())

    tot = mz[0]
    for z in range(1, ngz):
        tot = tot + mz[z]
    scale = lax.rsqrt(tot[1:2, :] / (epochs * tot[2:3, :]) + EPS)

    def over_gz(ref, *index):
        value = ref[index + (0,)]
        for z in range(1, ngz):
            value = value + ref[index + (z,)]
        return value

    centre = over_gz(sc) * scale
    surf[:, HX:HX + lx, 0:LANES] = centre
    surf_out[...] = centre
    surf[:, 0:HX, 0:LANES] = over_gz(sx, 0) * scale
    surf[:, HX + lx:, 0:LANES] = over_gz(sx, 1) * scale
    edge_lane = (lane8 < 8) | (lane8 >= LANES - 8)
    for d in range(3):
        from_left = over_gz(sy, d, 0)
        from_right = over_gz(sy, d, 1)
        for c in range(3):
            for r in ((groups - 1,), range(groups), (0,))[d]:
                k = c * groups + r
                q, kk = k // 8, k % 8
                tile = jnp.where(
                    lane8 < 64, lane_roll(from_right[q], -16 * kk),
                    lane_roll(from_left[q], 112 - 16 * kk),
                )
                row = (0, HX + r * 8, HX + lx)[d]
                surf[c, row:row + 8, LANES:width] = jnp.where(edge_lane, tile * scale, 0.0)

    row_i = lax.broadcasted_iota(jnp.int32, (rows_x, width), 0)
    col_i = lax.broadcasted_iota(jnp.int32, (rows_x, width), 1)
    inside_x = ((row_i >= HX) | (gx > 0)) & ((row_i < HX + lx) | (gx < ngx - 1))
    inside_y = (col_i < LANES) | ((col_i < LANES + 8) & (gy < ngy - 1)) | (
        (col_i >= width - 8) & (gy > 0)
    )
    mask = jnp.where(inside_x & inside_y, 1.0, 0.0)

    for c in range(3):
        s = surf[c]
        fields[c] = (6.0 - SHIFT) * s - (up(s, 0) + down(s, 0)) - (up(s, 1) + down(s, 1))
    s0, s1, s2 = surf[0], surf[1], surf[2]
    flux = mask * 0.5 * ((up(s0, 0) - down(s0, 0)) + (up(s1, 1) - down(s1, 1)))
    fields[3] = flux
    fields[4] = 0.5 * (up(flux, 0) - down(flux, 0))
    fields[5] = 0.5 * (up(s2, 0) - down(s2, 0))
    fields[6] = 0.5 * (up(flux, 1) - down(flux, 1))
    fields[7] = 0.5 * (up(s2, 1) - down(s2, 1))
    fields[8] = mask

    z_all = nz * ngz

    def inside_z(z):
        return jnp.where((z >= 0) & (z < z_all), 1.0, 0.0).astype(F32)

    first_z = gz * nz

    def apply_first(iz, carry):
        zg = first_z + iz - 4
        dmm, dm, d0, dp, dpp = [dext[iz + j][0:1, 0:1] for j in range(5)]
        here = inside_z(zg)
        e0 = 0.5 * here * (dp - dm)
        ep = 0.5 * inside_z(zg + 1) * (dpp - d0)
        em = 0.5 * inside_z(zg - 1) * (d0 - dmm)
        k = kext[iz]
        m = fields[8] * here
        kd = k * d0 - (dm + dp)
        v1[0, iz] = m * (d0 * fields[0] + kd * surf[0]
                         - KAPPA * (d0 * fields[4] + e0 * fields[5]))
        v1[1, iz] = m * (d0 * fields[1] + kd * surf[1]
                         - KAPPA * (d0 * fields[6] + e0 * fields[7]))
        v1[2, iz] = m * (d0 * fields[2] + kd * surf[2]
                         - (0.5 * KAPPA) * ((dp - dm) * fields[3] + (ep - em) * surf[2]))
        return carry

    lax.fori_loop(0, nz + 8, apply_first, 0)

    def again(source, planes, store):
        offset = (nz - planes) // 2

        def spread_of(iz, carry):
            zg = first_z + offset + iz - 1
            a = source[0, iz + 1]
            b = source[1, iz + 1]
            w = (up(a, 0) - down(a, 0)) + (up(b, 1) - down(b, 1))
            w = w + (source[2, iz + 2] - source[2, iz])
            div[iz] = (0.5 * inside_z(zg)) * fields[8] * w
            return carry

        lax.fori_loop(0, planes + 2, spread_of, 0)

        def image_of(iz, carry):
            zg = first_z + offset + iz
            k = kext[iz + offset + 4] + (6.0 - SHIFT)
            here = div[iz + 1]
            slopes = (
                up(here, 0) - down(here, 0),
                up(here, 1) - down(here, 1),
                div[iz + 2] - div[iz],
            )
            m = inside_z(zg) * fields[8]
            for c in range(3):
                a = source[c, iz + 2]
                near = (up(a, 0) + down(a, 0)) + (up(a, 1) + down(a, 1))
                near = near + (source[c, iz + 1] + source[c, iz + 3])
                store(c, iz, m * (k * a - near - (0.5 * KAPPA) * slopes[c]))
            return carry

        lax.fori_loop(0, planes, image_of, 0)

    def store2(c, iz, value):
        v2[c, iz] = value

    def store3(c, iz, value):
        v3[c, iz] = value[HX:HX + lx, 0:LANES]

    def emit(src, out, number):
        return pltpu.make_async_copy(src, out, out_sem.at[number])

    outs = [
        emit(v1.at[:, pl.ds(4, nz), pl.ds(HX, lx), pl.ds(0, LANES)], v1_out, 0),
        emit(v2.at[:, pl.ds(2, nz), pl.ds(HX, lx), pl.ds(0, LANES)], v2_out, 1),
        emit(v3, v3_out, 2),
    ]
    outs[0].start()
    again(v1, nz + 4, store2)
    outs[1].start()
    again(v2, nz, store3)
    outs[2].start()

    def fold(a):
        return jnp.sum(a.reshape(lx // 8, 8, LANES), axis=0)

    def products(iz, acc):
        d0 = dext[iz + 6][0:1, 0:1]
        acc = list(acc)
        for c in range(3):
            a0 = d0 * surf[c, HX:HX + lx, 0:LANES]
            a1 = v1[c, iz + 4, HX:HX + lx, 0:LANES]
            a2 = v2[c, iz + 2, HX:HX + lx, 0:LANES]
            a3 = v3[c, iz]
            for i, (a, b) in enumerate(
                ((a0, a0), (a0, a1), (a1, a1), (a1, a2), (a2, a2), (a2, a3))
            ):
                acc[i] = acc[i] + fold(a * b)
        return tuple(acc)

    acc = lax.fori_loop(0, nz, products, tuple([jnp.zeros((8, LANES), F32)] * 6))
    sub8 = lax.broadcasted_iota(jnp.int32, (8, LANES), 0)
    packed = jnp.zeros((8, LANES), F32)
    for i in range(6):
        packed = jnp.where(sub8 == i, jnp.sum(acc[i], axis=0, keepdims=True), packed)
    momsend[...] = packed
    mom[flat] = packed
    reduces = []
    for t in range(1, total):
        p, device = peer_of(t)
        q = lax.rem(flat + total - t, total)
        out = copy(momsend, mom.at[flat], r_send.at[t], r_recv.at[flat], device)
        out.start()
        reduces.append((out, copy(momsend, mom.at[q], r_send.at[t], r_recv.at[q], device)))
    for _, came in reduces:
        came.wait_recv()
    added = mom[0]
    for t in range(1, total):
        added = added + mom[t]
    mu = jnp.sum(added, axis=1, keepdims=True)
    mu = [jnp.broadcast_to(mu[i:i + 1, :], (1, LANES)) for i in range(6)]

    def inner(a, b):
        out = None
        for i, p in enumerate(a):
            for j, r in enumerate(b):
                if p is None or r is None:
                    continue
                term = p * r * mu[i + j]
                out = term if out is None else out + term
        return out

    def plus(a, factor, b):
        out = []
        for p, r in zip(a, b):
            if r is None:
                out.append(p)
            elif p is None:
                out.append(factor * r)
            else:
                out.append(p + factor * r)
        return out

    one = jnp.ones((1, LANES), F32)
    x = [None] * 4
    r = [one, None, None, None]
    p = [one, None, None, None]
    rr = mu[0]
    for step in range(ITERS):
        ap = [None] + p[:3]
        ap = plus(ap, SHIFT * one, p)
        alpha = rr / inner(p, ap)
        x = plus(x, alpha, p)
        r = plus(r, -alpha, ap)
        if step + 1 < ITERS:
            new = inner(r, r)
            p = plus(r, new / rr, p)
            rr = new
    rows = x[:3] + r
    result = jnp.zeros((8, LANES), F32)
    for i, value in enumerate(rows):
        result = jnp.where(sub8 == i, value, result)
    coef_out[...] = result

    for data, note, _, _ in exchange:
        data.wait_send()
        note.wait_send()
    for there, out in sends:
        if there is None:
            out.wait_send()
        else:
            pl.when(there)(lambda out=out: out.wait_send())
    for out, _ in reduces:
        out.wait_send()
    for out in outs:
        out.wait()


def per_device(
    ngx, ngy, ngz,
    observed, predicted, coherence_mask, block_count, block_owner,
    block_matrix_choice, block_patch, look_vector, interp_weights, depth_kernel, stiffness,
):
    blocks, epochs, pixels = observed.shape
    owners = ngx * ngy
    total = owners * ngz
    cap = max(8, 2 * blocks // owners)
    nz, lx, ly = stiffness.shape
    rows_x = lx + 2 * HX
    width = 2 * LANES
    cells = PATCH_X * PATCH_Y
    meta_w = -(-owners * cap // LANES) * LANES
    packs = -(-3 * lx // 64)
    column = lax.broadcasted_iota(jnp.int32, (blocks, pixels), 1)
    valid = coherence_mask.astype(F32) * (column < block_count[:, None]).astype(F32)
    resid = (predicted - observed) * valid[:, None, :]
    partial = jnp.stack([jnp.sum(resid * resid), jnp.sum(valid)])
    coeffs = jnp.stack(
        [sum(look_vector[e, c] * resid[:, e, :] for e in range(epochs)) for c in range(3)], axis=1
    ).astype(BF16)
    coeffs = jnp.pad(coeffs, ((0, 0), (0, 5), (0, 0)))
    vmem = pl.BlockSpec(memory_space=pltpu.VMEM)
    smem = pl.BlockSpec(memory_space=pltpu.SMEM)
    hbm = pl.BlockSpec(memory_space=pl.ANY)
    dma = pltpu.SemaphoreType.DMA
    field = jax.ShapeDtypeStruct((3, nz, lx, ly), F32)

    def buf(*shape):
        return pltpu.VMEM(shape, F32)

    v1, v2, v3, surf, coef = pl.pallas_call(
        functools.partial(body, ngx, ngy, ngz, cap, epochs),
        out_shape=[field, field, field,
                   jax.ShapeDtypeStruct((3, lx, ly), F32),
                   jax.ShapeDtypeStruct((8, LANES), F32)],
        in_specs=[smem, smem, smem, vmem, vmem, vmem, vmem, vmem],
        out_specs=[hbm, hbm, hbm, vmem, vmem],
        scratch_shapes=[
            buf(blocks, 8, cells),
            buf(owners, 3 * cap, cells),
            buf(owners, 8, meta_w),
            buf(owners, 3 * cap, cells),
            buf(owners, 8, meta_w),
            buf(3, lx, ly),
            buf(2, packs, 8, LANES),
            buf(8, LANES),
            buf(2, ngz, 3, 8, LANES),
            buf(3, 2, ngz, packs, 8, LANES),
            buf(ngz, 3, lx, ly),
            buf(ngz, 8, LANES),
            buf(nz + 12, 8, LANES),
            buf(nz + 8, rows_x, width),
            buf(2, nz // 8, rows_x, LANES),
            buf(2, nz // 8, rows_x, LANES),
            buf(3, rows_x, width),
            buf(3, nz + 8, rows_x, width),
            buf(3, nz + 4, rows_x, width),
            buf(3, nz, lx, ly),
            buf(nz + 6, rows_x, width),
            buf(9, rows_x, width),
            buf(8, LANES),
            buf(total, 8, LANES),
            dma((owners,)), dma((owners,)), dma((owners,)), dma((owners,)),
            dma((4,)), dma((4,)), dma((4,)), dma((4,)),
            dma((2 * ngz + 8 * ngz,)),
            dma((2, ngz)), dma((3, 2, ngz)), dma((ngz,)), dma((ngz,)),
            dma((total,)), dma((total,)), dma((3,)),
        ],
        compiler_params=pltpu.CompilerParams(
            collective_id=0, has_side_effects=True, vmem_limit_bytes=48 * 1024 * 1024
        ),
    )(
        block_matrix_choice, depth_kernel, partial, block_owner, block_patch[:, None],
        coeffs, interp_weights, stiffness,
    )
    c = coef[:, 0]
    v0 = depth_kernel[None, :, None, None] * surf[:, None, :, :]
    adjoint_field = c[0] * v0 + c[1] * v1 + c[2] * v2
    cg_residual = c[3] * v0 + c[4] * v1 + c[5] * v2 + c[6] * v3
    return adjoint_field, cg_residual


def solution(mesh):
    spread = P(("grp", "gx", "gy", "gz"))
    in_specs = (
        P(("grp", "gx", "gy", "gz"), None, None),
        P(("grp", "gx", "gy", "gz"), None, None),
        P(("grp", "gx", "gy", "gz"), None),
        spread,
        P(("grp", "gx", "gy", "gz"), None),
        spread,
        spread,
        P(),
        P(),
        P(("grp", "gz")),
        P(("grp", "gz"), "gx", "gy"),
    )
    out_specs = (P(None, ("grp", "gz"), "gx", "gy"), P(None, ("grp", "gz"), "gx", "gy"))
    step = functools.partial(per_device, mesh.shape["gx"], mesh.shape["gy"], mesh.shape["gz"])
    return jax.shard_map(
        step, mesh=mesh, in_specs=in_specs, out_specs=out_specs, check_vma=False
    )
```

time: 351 us -> 66.1 us (0.19)
  blocking collectives: 130 us -> 0 us
  waiting for transfers between devices: 73.2 us -> 0 us
  starting transfers between devices: 70.3 us -> 0 us
  Pallas kernels: 0 us -> 41.2 us
  local copies, waits for them, and re-layouts: 26.9 us -> 4.85 us
  between operations: 12.4 us -> 0.72 us
  matrix products: 10.8 us -> 0 us
  other arithmetic: 26.2 us -> 18.9 us
    psum x5 -> x0, blocking collectives: 130 us -> none  [the longest x3 91.4 us: two_products(): lax.psum((jnp.sum(residual * residual), jnp.sum(residual * image)), ('gx'...]
    ppermute x36 -> x0, waiting for transfers between devices: 65.7 us -> none  [the longest x18 55 us: extended(): lax.ppermute(head, axis, [((i + 1) % count, i) for i in range(ends)])]
    ppermute x36 -> x0, starting transfers between devices: 55.9 us -> none  [the longest x18 32.4 us: extended(): lax.ppermute(tail, axis, [(i, (i + 1) % count) for i in range(ends)])]
    pallas_call x0 -> x1, Pallas kernels: none -> 41.2 us  [per_device(): pl.pallas_call(functools.partial(body, ngx, ngy, ngz, cap, epochs), out_s...]
    all_to_all x3 -> x0, starting transfers between devices: 14.4 us -> none  [the longest x1 7.28 us: per_device(): lax.all_to_all(table_slot, ('gx', 'gy'), split_axis=0, concat_axis=0, til...]
    dot_general x7 -> x0, matrix products: 10.8 us -> none  [the longest x4 8.3 us: per_group(): jnp.einsum('aow,awv->aov', block_coefficient_values, selected_entries, pr...]
    gather x4 -> x0, local copies, waits for them, and re-layouts: 8.72 us -> none  [per_group(): selected_entries = jnp.take(weights, block_tables, axis=0)]
    all_to_all x3 -> x0, waiting for transfers between devices: 7.46 us -> none  [the longest x1 5.1 us: per_device(): lax.all_to_all(patch_slot, ('gx', 'gy'), split_axis=0, concat_axis=0, til...]
  transfers between devices with their start and end apart: 39 -> 0, of which waited for: 25 -> 0; matrix products, arithmetic and copies ran while one was open for 4% -> 0% of each run, Pallas kernels for 0% -> 0%
where the time goes in v1:
time: 66.1 us; the launch traced here: 65.7 us
  Pallas kernels  41.2 us (62%)
  other arithmetic  18.9 us (29%)
  local copies, waits for them, and re-layouts  4.85 us (7%)
  between operations  0.72 us (1%)
    pallas_call x1, Pallas kernels, per_device(): pl.pallas_call(functools.partial(body, ngx, ngy, ngz, cap, epochs), out_s...  41.2 us
    another operation x2, other arithmetic  8.05 us
    add x1, other arithmetic, per_device(): cg_residual = c[3] * v0 + c[4] * v1 + c[5] * v2 + c[6] * v3  5.92 us
    reduce_sum x2, other arithmetic, per_device(): partial = jnp.stack([jnp.sum(resid * resid), jnp.sum(valid)])  3.32 us
    slice x1, local copies, waits for them, and re-layouts, per_device(): look_vector[e, c] * resid[:, e, :]  1.8 us
    unnamed x9, local copies, waits for them, and re-layouts  1.7 us
    another operation x1, other arithmetic, per_device(): partial = jnp.stack([jnp.sum(resid * resid), jnp.sum(valid)])  1.37 us

profile of v1, /device:TPU:0, one launch (start us, length us, event | category | flops | bytes accessed | tf_op | source)
XLA Modules:
  0.0 65.7 jit_solution(14870750249619454001)
XLA Ops:
  0.6 0.0 copy-start.2
  0.6 0.0 copy-start
  0.7 0.0 copy-start.3
  0.7 1.8 %fusion.12 = (f32[1,1]{1,0:T(1,128)}, f32[1,1]{1,0:T(1,128)}, f32[1,1]{1,0:T(1,128)}, f32[1,1]{1,0:T(1,128)}, f32[1,1]{1,0:T(1,128)}, /*index=5*/f32[1,1]{1,0:T(...) fusion(f32[4,3]{1,0:T(4,128)} %param.18), kind=kLoop, calls=%fused_computation.23 | loop fusion | bytes 96 | tf_op jit(solution)/shard_map/slice | solution.py:570
  2.5 0.7 %copy.18.owner_ref = s32[64,1]{1,0:T(8,128)S(1)} copy(s32[64,1]{0,1:T(1,128)} %param.15) | data formatting | bytes 512 | tf_op args[4]
  3.2 0.7 %copy.19.patch_ref = s32[64,1]{1,0:T(8,128)S(1)} copy(s32[64,1]{0,1:T(1,128)} %bitcast.22) | data formatting | bytes 512 | tf_op jit(solution)/shard_map/broadcast_in_dim | solution.py:624
  4.0 1.5 %fusion.10 = (f32[]{:T(128)}, f32[64,256]{1,0:T(8,128)S(1)}) fusion(s32[64,256]{1,0:T(8,128)} %param.13, s32[64]{0:T(128)} %param.14), kind=kLoop, calls=%fused_computation.21 | loop fusion | flops 65535 | bytes 131332 | tf_op jit(solution)/shard_map/reduce_sum | solution.py:568
  5.5 1.8 %multiply_reduce_fusion = (f32[]{:T(128)}, f32[64,4,256]{2,1,0:T(4,128)S(1)}) fusion(f32[64,256]{1,0:T(8,128)S(1)} %get-tuple-element.15, f32[64,4,256]{2,1,0:T(4,128)} %param.12, f32[64,4,256]{2,1,0:T(4,128)} %param.11), kind=kLoop, calls=%fused_computation.13 | loop fusion | flops 262143 | bytes 851972 | tf_op jit(solution)/shard_map/reduce_sum | solution.py:568
  7.3 1.4 %pad_maximum_fusion.partial = f32[2]{0:T(128)S(1)} fusion(f32[1]{0:T(128)} %bitcast.1, f32[1]{0:T(128)} %bitcast), kind=kLoop, calls=%fused_computation.20 | loop fusion | flops 2 | bytes 16 | tf_op jit(solution)/shard_map/stack | solution.py:568
  8.6 2.8 %add_convert_fusion.1 = bf16[64,1,256]{2,1,0:T(2,128)(2,1)S(1)} fusion(f32[]{:T(128)} %bitcast.7, f32[]{:T(128)} %bitcast.10, f32[]{:T(128)} %bitcast.9, f32[]{:T(128)} %bitcast.8, f32[64,4,256]{2,1,0:T(4,128)S(1)} %get-tuple-element.13), kind=kLoop, calls=%fused_computation.16 | loop fusion | flops 131072 | bytes 294928 | tf_op jit(solution)/shard_map/convert.1
  11.4 5.3 %add_convert_fusion.2 = (bf16[64,1,256]{2,1,0:T(2,128)(2,1)S(1)}, bf16[64,1,256]{2,1,0:T(2,128)(2,1)S(1)}) fusion(f32[]{:T(128)} %bitcast.3, f32[]{:T(128)} %bitcast.6, f32[]{:T(128)} %bitcast.5, f32[]{:T(128)} %bitcast.4, f32[64,4,256]{2,1,0:T(4,128)S(1)} %get-tuple-element.13, f32[]{:T(128)} %bitcast.14, f32[]{:T(128)} %bitcast.13, f32[]{:T(128)} %bitcast.12, ...), kind=kLoop, calls=%fused_computation.17 | loop fusion | flops 262144 | bytes 327712 | tf_op jit(solution)/shard_map/convert
  16.7 0.3 fusion.9.coeffs
  17.0 0.0 copy-done.2
  17.0 0.0 copy-done
  17.0 0.0 copy-done.3
  17.0 0.0 copy-start.1
  17.0 0.9 %copy-done.1 = f32[16,32,128]{2,1,0:T(8,128)S(1)} copy-done((f32[16,32,128]{2,1,0:T(8,128)S(1)}, f32[16,32,128]{2,1,0:T(8,128)}, u32[]{:S(2)}) %copy-start.1) | copy-done | bytes 262168
  18.0 41.2 %shard_map.122 = (f32[3,16,32,128]{3,2,1,0:T(8,128)S(1)}, f32[3,16,32,128]{3,2,1,0:T(8,128)S(1)}, f32[3,16,32,128]{3,2,1,0:T(8,128)S(1)}, f32[3,32,128]{2,1,0:T(8,128)S(1)}, f32[8,128]{1,0:T(8,128)S(1)}) custom-call(s32[64]{0:T(128)S(1)} %copy-done.3, f32[16]{0:T(128)S(1)} %copy-done.2, f32[2]{0:T(128)S(1)} %pad_maximum_fusion.partial, ...), custom_call_target="tpu_custom_call" | custom-call | tf_op jit(solution)/shard_map/pallas_call | solution.py:582
  59.2 0.6 fusion.11
  59.8 5.9 %fusion.4 = (f32[3,16,32,128]{3,2,1,0:T(8,128)}, f32[3,16,32,128]{3,2,1,0:T(8,128)}) fusion(f32[3,16,32,128]{3,2,1,0:T(8,128)S(1)} %get-tuple-element.11, f32[3,16,32,128]{3,2,1,0:T(8,128)S(1)} %get-tuple-element.10, f32[3,16,32,128]{3,2,1,0:T(8,128)S(1)} %get-tuple-element.9, f32[]{:T(128)} %bitcast.21, f32[]{:T(128)} %bitcast.20, f32[]{:T(128)} %bitcast.19, ...), kind=kLoop, calls=%fused_computation.6 | loop fusion | flops 2555904 | bytes 3981404 | tf_op jit(solution)/shard_map/add | solution.py:630
Async XLA Ops:
  0.6 16.3 %copy-start.2 = (f32[16]{0:T(128)S(1)}, f32[16]{0:T(128)}, u32[]{:S(2)}) copy-start(f32[16]{0:T(128)} %depth.1) | copy-start | bytes 196
  0.6 16.3 %copy-start = (bf16[32,256,128]{2,1,0:T(8,128)(2,1)S(1)}, bf16[32,256,128]{2,1,0:T(8,128)(2,1)}, u32[]{:S(2)}) copy-start(bf16[32,256,128]{2,1,0:T(8,128)(2,1)} %weights.1) | copy-start | bytes 6291460
  0.7 16.3 %copy-start.3 = (s32[64]{0:T(128)S(1)}, s32[64]{0:T(128)}, u32[]{:S(2)}) copy-start(s32[64]{0:T(128)} %choice.1) | copy-start | bytes 772
  17.0 1.0 %copy-start.1 = (f32[16,32,128]{2,1,0:T(8,128)S(1)}, f32[16,32,128]{2,1,0:T(8,128)}, u32[]{:S(2)}) copy-start(f32[16,32,128]{2,1,0:T(8,128)} %stiff.1) | copy-start | bytes 786436

commit v2 on v1

--- a/solution.py
+++ b/solution.py
@@ -15,6 +15,7 @@
 SHIFT = 8.0
 HX = 8
 LANES = 128
+VMEM_ALL = 67043328
 MESH = pl.DeviceIdType.MESH
 F32 = jnp.float32
 BF16 = jnp.bfloat16
@@ -51,8 +52,10 @@
 
 def body(
     ngx, ngy, ngz, cap, epochs,
-    choice, depth, partial, owner_ref, patch_ref, coeffs, weights, stiff,
+    choice, depth, look, owner_ref, patch_ref, count_ref, mask_ref,
+    observed_hbm, predicted_hbm, weights_hbm, stiff_hbm,
     v1_out, v2_out, v3_out, surf_out, coef_out,
+    observed, predicted, weights, usable, coeffs, in_sem,
     sums, send, meta, recv, metarecv, part, ppk, msum, sx, sy, sc, mz,
     dext, kext, pk, pkrecv, surf, v1, v2, v3, div, fields, momsend, mom,
     a_send, a_recv, m_send, m_recv, kx_sem, ky_sem, kz_sem, dz_sem,
@@ -65,7 +68,7 @@
     total = owners * ngz
     me = gx * ngy + gy
     flat = me * ngz + gz
-    nz, lx, ly = stiff.shape
+    nz, lx, ly = stiff_hbm.shape
     blocks = choice.shape[0]
     rows_x = lx + 2 * HX
     width = 2 * LANES
@@ -99,21 +102,113 @@
             device_id=device, device_id_type=MESH,
         )
 
-    for b in range(blocks):
-        table = weights[choice[b]]
-        sums[b] = jnp.dot(coeffs[b], table, preferred_element_type=F32)
-
+    core = kext.at[pl.ds(4, nz), pl.ds(HX, lx), pl.ds(0, LANES)]
+    loads = [
+        pltpu.make_async_copy(src, dst, in_sem.at[i])
+        for i, (src, dst) in enumerate((
+            (observed_hbm, observed), (predicted_hbm, predicted),
+            (stiff_hbm, core), (weights_hbm, weights),
+        ))
+    ]
+    for load in loads:
+        load.start()
+
+    rows_i = lax.broadcasted_iota(jnp.int32, (blocks, blocks), 0)
+    cols_i = lax.broadcasted_iota(jnp.int32, (blocks, blocks), 1)
+
+    def column_of(row):
+        wide = jnp.broadcast_to(row, (blocks, blocks))
+        return jnp.sum(jnp.where(rows_i == cols_i, wide, 0), axis=1, keepdims=True)
+
+    pixels = mask_ref.shape[1]
+    pixel = lax.broadcasted_iota(jnp.int32, (blocks, pixels), 1)
+    valid = jnp.where(pixel < column_of(count_ref[...]), mask_ref[...], 0).astype(F32)
+    usable[...] = valid
+
+    def total_of(a):
+        return jnp.sum(jnp.sum(a, axis=0, keepdims=True), axis=1, keepdims=True)
+
+    weight = total_of(valid)
     for z in range(nz):
         dext[z + 6] = jnp.full((8, LANES), depth[z], F32)
-    kext[4:4 + nz, HX:HX + lx, 0:LANES] = stiff[...]
-
-    owner_col = owner_ref[...]
-    patch_col = patch_ref[...]
-    rows_i = lax.broadcasted_iota(jnp.int32, (blocks, blocks), 0)
-    cols_i = lax.broadcasted_iota(jnp.int32, (blocks, blocks), 1)
-    owner_wide = jnp.broadcast_to(owner_col, (blocks, blocks))
-    owner_row = jnp.sum(jnp.where(rows_i == cols_i, owner_wide, 0), axis=0, keepdims=True)
-    same = owner_wide == owner_row
+    component = lax.broadcasted_iota(jnp.int32, (8, pixels), 0)
+    views = []
+    for e in range(epochs):
+        view = jnp.zeros((8, pixels), F32)
+        for c in range(3):
+            view = jnp.where(component == c, look[e, c], view)
+        views.append(view)
+
+    loads[0].wait()
+    loads[1].wait()
+    squares = jnp.zeros((epochs, pixels), F32)
+    for b in range(blocks):
+        resid = (predicted[b] - observed[b]) * jnp.broadcast_to(
+            usable[b:b + 1, :], (epochs, pixels)
+        )
+        squares = squares + resid * resid
+        seen = None
+        for e in range(epochs):
+            term = jnp.broadcast_to(resid[e:e + 1, :], (8, pixels)) * views[e]
+            seen = term if seen is None else seen + term
+        coeffs[b] = seen.astype(BF16)
+    misfit = total_of(squares)
+
+    loads[2].wait()
+    pl.semaphore_wait(barrier, total - 1)
+
+    def both_sides(position, count, axis, low_src, low_dst, high_src, high_dst, sem, fill):
+        others = {"gx": gx, "gy": gy, "gz": gz}
+        lower, upper = dict(others), dict(others)
+        lower[axis] = position - 1
+        upper[axis] = position + 1
+        to_low = copy(low_src, high_dst, sem.at[0], sem.at[1], lower)
+        to_high = copy(high_src, low_dst, sem.at[2], sem.at[3], upper)
+        has_low = position > 0
+        has_high = position < count - 1
+        pl.when(has_low)(lambda: to_low.start())
+        pl.when(has_high)(lambda: to_high.start())
+        pl.when(jnp.logical_not(has_low))(lambda: fill(low_dst))
+        pl.when(jnp.logical_not(has_high))(lambda: fill(high_dst))
+
+        def finish():
+            @pl.when(has_low)
+            def _():
+                to_low.wait_send()
+                copy(low_src, low_dst, sem.at[2], sem.at[3], lower).wait_recv()
+
+            @pl.when(has_high)
+            def _():
+                to_high.wait_send()
+                copy(high_src, high_dst, sem.at[0], sem.at[1], upper).wait_recv()
+
+        return finish
+
+    def zero(ref):
+        ref[...] = jnp.zeros(ref.shape, F32)
+
+    finish_x = both_sides(
+        gx, ngx, "gx",
+        kext.at[pl.ds(4, nz), pl.ds(HX, HX), pl.ds(0, LANES)],
+        kext.at[pl.ds(4, nz), pl.ds(0, HX), pl.ds(0, LANES)],
+        kext.at[pl.ds(4, nz), pl.ds(lx, HX), pl.ds(0, LANES)],
+        kext.at[pl.ds(4, nz), pl.ds(HX + lx, HX), pl.ds(0, LANES)],
+        kx_sem, zero,
+    )
+    finish_d = both_sides(
+        gz, ngz, "gz",
+        dext.at[pl.ds(6, 6)], dext.at[pl.ds(0, 6)],
+        dext.at[pl.ds(nz, 6)], dext.at[pl.ds(nz + 6, 6)],
+        dz_sem, zero,
+    )
+
+    loads[3].wait()
+    for b in range(blocks):
+        sums[b] = jnp.dot(coeffs[b], weights[choice[b]], preferred_element_type=F32)
+
+    owner_row = owner_ref[...]
+    patch_col = column_of(patch_ref[...])
+    same = column_of(owner_row) == owner_row
     rank_row = jnp.sum(jnp.where(same & (rows_i < cols_i), 1, 0), axis=0, keepdims=True)
     rank_col = jnp.sum(jnp.where(same & (cols_i < rows_i), 1, 0), axis=1, keepdims=True)
     slot_row = owner_row * cap + rank_row
@@ -128,12 +223,10 @@
     owner_hot = jnp.where(owner_ids == owner_row, 1.0, 0.0).astype(BF16)
     patches = jnp.dot(owner_hot, ranked, preferred_element_type=F32)
     sub_ids = lax.broadcasted_iota(jnp.int32, (8, meta_w), 0)
-    extras = jnp.where(sub_ids == 1, partial[0], jnp.where(sub_ids == 2, partial[1], 0.0))
+    extras = jnp.where(sub_ids == 1, misfit, jnp.where(sub_ids == 2, weight, 0.0))
     for o in range(owners):
         line = jnp.broadcast_to(patches[o:o + 1, :], (8, meta_w))
         meta[o] = jnp.where(sub_ids == 0, line, extras)
-
-    pl.semaphore_wait(barrier, total - 1)
 
     exchange = []
     for t in range(1, owners):
@@ -150,50 +243,6 @@
             copy(meta.at[o], metarecv.at[src], m_send.at[t], m_recv.at[src], device),
         ))
 
-    def both_sides(position, count, axis, low_src, low_dst, high_src, high_dst, sem, fill):
-        others = {"gx": gx, "gy": gy, "gz": gz}
-        lower, upper = dict(others), dict(others)
-        lower[axis] = position - 1
-        upper[axis] = position + 1
-        to_low = copy(low_src, high_dst, sem.at[0], sem.at[1], lower)
-        to_high = copy(high_src, low_dst, sem.at[2], sem.at[3], upper)
-        has_low = position > 0
-        has_high = position < count - 1
-        pl.when(has_low)(lambda: to_low.start())
-        pl.when(has_high)(lambda: to_high.start())
-        pl.when(jnp.logical_not(has_low))(lambda: fill(low_dst))
-        pl.when(jnp.logical_not(has_high))(lambda: fill(high_dst))
-
-        def finish():
-            @pl.when(has_low)
-            def _():
-                to_low.wait_send()
-                copy(low_src, low_dst, sem.at[2], sem.at[3], lower).wait_recv()
-
-            @pl.when(has_high)
-            def _():
-                to_high.wait_send()
-                copy(high_src, high_dst, sem.at[0], sem.at[1], upper).wait_recv()
-
-        return finish
-
-    def zero(ref):
-        ref[...] = jnp.zeros(ref.shape, F32)
-
-    finish_x = both_sides(
-        gx, ngx, "gx",
-        stiff.at[:, pl.ds(0, HX), :],
-        kext.at[pl.ds(4, nz), pl.ds(0, HX), pl.ds(0, LANES)],
-        stiff.at[:, pl.ds(lx - HX, HX), :],
-        kext.at[pl.ds(4, nz), pl.ds(HX + lx, HX), pl.ds(0, LANES)],
-        kx_sem, zero,
-    )
-    finish_d = both_sides(
-        gz, ngz, "gz",
-        dext.at[pl.ds(6, 6)], dext.at[pl.ds(0, 6)],
-        dext.at[pl.ds(nz, 6)], dext.at[pl.ds(nz + 6, 6)],
-        dz_sem, zero,
-    )
     finish_x()
     lane1 = lax.broadcasted_iota(jnp.int32, (rows_x, LANES), 1)
     for g in range(nz // 8):
@@ -209,21 +258,6 @@
     finish_y = both_sides(
         gy, ngy, "gy", pk.at[0], pkrecv.at[0], pk.at[1], pkrecv.at[1], ky_sem, zero
     )
-    finish_y()
-    for g in range(nz // 8):
-        from_left = pkrecv[0, g]
-        from_right = pkrecv[1, g]
-        for k in range(8):
-            kext[4 + 8 * g + k, :, LANES:width] = jnp.where(
-                lane1 < 64, lane_roll(from_right, -16 * k), lane_roll(from_left, 112 - 16 * k)
-            )
-    finish_z = both_sides(
-        gz, ngz, "gz",
-        kext.at[pl.ds(4, 4)], kext.at[pl.ds(0, 4)],
-        kext.at[pl.ds(nz, 4)], kext.at[pl.ds(nz + 4, 4)],
-        kz_sem, zero,
-    )
-
     recv[me] = send[me]
     metarecv[me] = meta[me]
     for data, note, data_in, note_in in exchange:
@@ -314,7 +348,21 @@
     sc[gz] = part[...]
     mz[gz] = msum[...]
     finish_d()
-    finish_z()
+    finish_y()
+    for g in range(nz // 8):
+        from_left = pkrecv[0, g]
+        from_right = pkrecv[1, g]
+        for k in range(8):
+            kext[4 + 8 * g + k, :, LANES:width] = jnp.where(
+                lane1 < 64, lane_roll(from_right, -16 * k), lane_roll(from_left, 112 - 16 * k)
+            )
+    finish_z = both_sides(
+        gz, ngz, "gz",
+        kext.at[pl.ds(4, 4)], kext.at[pl.ds(0, 4)],
+        kext.at[pl.ds(nz, 4)], kext.at[pl.ds(nz + 4, 4)],
+        kz_sem, zero,
+    )
+
     for there, came in receives:
         if there is None:
             came.wait_recv()
@@ -397,6 +445,7 @@
                          - (0.5 * KAPPA) * ((dp - dm) * fields[3] + (ep - em) * surf[2]))
         return carry
 
+    finish_z()
     lax.fori_loop(0, nz + 8, apply_first, 0)
 
     def again(source, planes, store):
@@ -438,13 +487,13 @@
     def store3(c, iz, value):
         v3[c, iz] = value[HX:HX + lx, 0:LANES]
 
-    def emit(src, out, number):
-        return pltpu.make_async_copy(src, out, out_sem.at[number])
-
     outs = [
-        emit(v1.at[:, pl.ds(4, nz), pl.ds(HX, lx), pl.ds(0, LANES)], v1_out, 0),
-        emit(v2.at[:, pl.ds(2, nz), pl.ds(HX, lx), pl.ds(0, LANES)], v2_out, 1),
-        emit(v3, v3_out, 2),
+        pltpu.make_async_copy(src, dst, out_sem.at[i])
+        for i, (src, dst) in enumerate((
+            (v1.at[:, pl.ds(4, nz), pl.ds(HX, lx), pl.ds(0, LANES)], v1_out),
+            (v2.at[:, pl.ds(2, nz), pl.ds(HX, lx), pl.ds(0, LANES)], v2_out),
+            (v3, v3_out),
+        ))
     ]
     outs[0].start()
     again(v1, nz + 4, store2)
@@ -546,6 +595,44 @@
     for out in outs:
         out.wait()
 
+def combine(
+    depth, coef, surf, v1_in, v2_in, v3_in, field_out, resid_out,
+    v1, v2, v3, field, resid, in_sem, sem,
+):
+    nz = v1.shape[1]
+    chunk = 4 if nz % 4 == 0 else 1
+    arriving = []
+    for start in range(0, nz, chunk):
+        part = pl.ds(start, chunk)
+        for i, (src, dst) in enumerate(((v1_in, v1), (v2_in, v2), (v3_in, v3))):
+            load = pltpu.make_async_copy(
+                src.at[:, part], dst.at[:, part], in_sem.at[i, start // chunk]
+            )
+            load.start()
+            arriving.append(load)
+    factors = [coef[i:i + 1, :] for i in range(7)]
+    copies = []
+    for start in range(0, nz, chunk):
+        for load in arriving[3 * (start // chunk):3 * (start // chunk) + 3]:
+            load.wait()
+        for z in range(start, start + chunk):
+            for c in range(3):
+                a0 = depth[z] * surf[c]
+                a1, a2 = v1[c, z], v2[c, z]
+                field[c, z] = factors[0] * a0 + factors[1] * a1 + factors[2] * a2
+                resid[c, z] = (factors[3] * a0 + factors[4] * a1) + (
+                    factors[5] * a2 + factors[6] * v3[c, z]
+                )
+        part = pl.ds(start, chunk)
+        for i, (src, dst) in enumerate(((field, field_out), (resid, resid_out))):
+            out = pltpu.make_async_copy(
+                src.at[:, part], dst.at[:, part], sem.at[i, start // chunk]
+            )
+            out.start()
+            copies.append(out)
+    for out in copies:
+        out.wait()
+
 
 def per_device(
     ngx, ngy, ngz,
@@ -562,17 +649,9 @@
     cells = PATCH_X * PATCH_Y
     meta_w = -(-owners * cap // LANES) * LANES
     packs = -(-3 * lx // 64)
-    column = lax.broadcasted_iota(jnp.int32, (blocks, pixels), 1)
-    valid = coherence_mask.astype(F32) * (column < block_count[:, None]).astype(F32)
-    resid = (predicted - observed) * valid[:, None, :]
-    partial = jnp.stack([jnp.sum(resid * resid), jnp.sum(valid)])
-    coeffs = jnp.stack(
-        [sum(look_vector[e, c] * resid[:, e, :] for e in range(epochs)) for c in range(3)], axis=1
-    ).astype(BF16)
-    coeffs = jnp.pad(coeffs, ((0, 0), (0, 5), (0, 0)))
     vmem = pl.BlockSpec(memory_space=pltpu.VMEM)
     smem = pl.BlockSpec(memory_space=pltpu.SMEM)
-    hbm = pl.BlockSpec(memory_space=pl.ANY)
+    hbm = pl.BlockSpec(memory_space=pltpu.HBM)
     dma = pltpu.SemaphoreType.DMA
     field = jax.ShapeDtypeStruct((3, nz, lx, ly), F32)
 
@@ -584,9 +663,15 @@
         out_shape=[field, field, field,
                    jax.ShapeDtypeStruct((3, lx, ly), F32),
                    jax.ShapeDtypeStruct((8, LANES), F32)],
-        in_specs=[smem, smem, smem, vmem, vmem, vmem, vmem, vmem],
+        in_specs=[smem, smem, smem, vmem, vmem, vmem, vmem, hbm, hbm, hbm, hbm],
         out_specs=[hbm, hbm, hbm, vmem, vmem],
         scratch_shapes=[
+            buf(blocks, epochs, pixels),
+            buf(blocks, epochs, pixels),
+            pltpu.VMEM(interp_weights.shape, BF16),
+            buf(blocks, pixels),
+            pltpu.VMEM((blocks, 8, pixels), BF16),
+            dma((4,)),
             buf(blocks, 8, cells),
             buf(owners, 3 * cap, cells),
             buf(owners, 8, meta_w),
@@ -618,17 +703,21 @@
             dma((total,)), dma((total,)), dma((3,)),
         ],
         compiler_params=pltpu.CompilerParams(
-            collective_id=0, has_side_effects=True, vmem_limit_bytes=48 * 1024 * 1024
+            collective_id=0, has_side_effects=True, vmem_limit_bytes=VMEM_ALL
         ),
     )(
-        block_matrix_choice, depth_kernel, partial, block_owner, block_patch[:, None],
-        coeffs, interp_weights, stiffness,
-    )
-    c = coef[:, 0]
-    v0 = depth_kernel[None, :, None, None] * surf[:, None, :, :]
-    adjoint_field = c[0] * v0 + c[1] * v1 + c[2] * v2
-    cg_residual = c[3] * v0 + c[4] * v1 + c[5] * v2 + c[6] * v3
-    return adjoint_field, cg_residual
+        block_matrix_choice, depth_kernel, look_vector, block_owner.reshape(1, blocks),
+        block_patch[None, :], block_count[None, :], coherence_mask,
+        observed, predicted, interp_weights, stiffness,
+    )
+    return pl.pallas_call(
+        combine,
+        out_shape=[field, field],
+        in_specs=[smem, vmem, vmem, hbm, hbm, hbm],
+        out_specs=[hbm, hbm],
+        scratch_shapes=[buf(3, nz, lx, ly)] * 5 + [dma((3, nz)), dma((2, nz))],
+        compiler_params=pltpu.CompilerParams(vmem_limit_bytes=VMEM_ALL),
+    )(depth_kernel, coef, surf, v1, v2, v3)
 
 
 def solution(mesh):

time: 66.1 us -> 43.8 us (0.66)
  other arithmetic: 18.9 us -> 0 us
  local copies, waits for them, and re-layouts: 4.85 us -> 0 us
  Pallas kernels: 41.2 us -> 42.8 us
    another operation x4 -> x0, other arithmetic: 9.69 us -> none
    add x1 -> x0, other arithmetic: 5.92 us -> none  [per_device(): cg_residual = c[3] * v0 + c[4] * v1 + c[5] * v2 + c[6] * v3]
    pallas_call x0 -> x1, Pallas kernels: none -> 4.01 us  [per_device(): pl.pallas_call(combine, out_shape=[field, field], in_specs=[smem, vmem, v...]
    reduce_sum x2 -> x0, other arithmetic: 3.32 us -> none  [per_device(): partial = jnp.stack([jnp.sum(resid * resid), jnp.sum(valid)])]
    slice x2 -> x0, local copies, waits for them, and re-layouts: 2.4 us -> none  [the longest x1 1.8 us: per_device(): look_vector[e, c] * resid[:, e, :]]
    pallas_call x1, Pallas kernels: 41.2 us -> 38.8 us  [per_device(): pl.pallas_call(functools.partial(body, ngx, ngy, ngz, cap, epochs), out_s...]
    unnamed x9 -> x0, local copies, waits for them, and re-layouts: 1.7 us -> none
    broadcast_in_dim x1 -> x0, local copies, waits for them, and re-layouts: 0.74 us -> none  [per_device(): block_patch[:, None]]
where the time goes in v2:
time: 43.8 us; the launch traced here: 43.5 us
  Pallas kernels  42.8 us (98%)
  between operations  0.64 us (1%)
    pallas_call x1, Pallas kernels, per_device(): pl.pallas_call(functools.partial(body, ngx, ngy, ngz, cap, epochs), out_s...  38.8 us
    pallas_call x1, Pallas kernels, per_device(): pl.pallas_call(combine, out_shape=[field, field], in_specs=[smem, vmem, v...  4.01 us

profile of v2, /device:TPU:0, one launch (start us, length us, event | category | flops | bytes accessed | tf_op | source)
XLA Modules:
  0.0 43.5 jit_solution(10185807665621243921)
XLA Ops:
  0.6 38.8 %shard_map.122 = (f32[3,16,32,128]{3,2,1,0:T(8,128)}, f32[3,16,32,128]{3,2,1,0:T(8,128)}, f32[3,16,32,128]{3,2,1,0:T(8,128)}, f32[3,32,128]{2,1,0:T(8,128)}, f32[8,128]{1,0:T(8,128)}) custom-call(s32[64]{0:T(128)} %choice.1, f32[16]{0:T(128)} %depth.3, f32[4,3]{1,0:T(4,128)} %look.1, s32[1,64]{1,0:T(1,128)} %bitcast.3, s32[1,64]{1,0:T(1,128)} %bitcast.4, ...), custom_call_target="tpu_custom_call" | custom-call | tf_op jit(solution)/shard_map/pallas_call | solution.py:661
  39.5 4.0 %shard_map.123 = (f32[3,16,32,128]{3,2,1,0:T(8,128)}, f32[3,16,32,128]{3,2,1,0:T(8,128)}) custom-call(f32[16]{0:T(128)} %depth.3, f32[8,128]{1,0:T(8,128)} %get-tuple-element.7.coef, f32[3,32,128]{2,1,0:T(8,128)} %get-tuple-element.8.surf, f32[3,16,32,128]{3,2,1,0:T(8,128)} %get-tuple-element.9.v1_in, f32[3,16,32,128]{3,2,1,0:T(8,128)} %get-tuple-element.10.v2_in, ...), custom_call_target="tpu_custom_call" | custom-call | tf_op jit(solution)/shard_map/pallas_call | solution.py:713

commit v3 on v2

--- a/solution.py
+++ b/solution.py
@@ -446,7 +446,7 @@
         return carry
 
     finish_z()
-    lax.fori_loop(0, nz + 8, apply_first, 0)
+    lax.fori_loop(0, nz + 8, apply_first, 0, unroll=2)
 
     def again(source, planes, store):
         offset = (nz - planes) // 2
@@ -460,7 +460,7 @@
             div[iz] = (0.5 * inside_z(zg)) * fields[8] * w
             return carry
 
-        lax.fori_loop(0, planes + 2, spread_of, 0)
+        lax.fori_loop(0, planes + 2, spread_of, 0, unroll=2)
 
         def image_of(iz, carry):
             zg = first_z + offset + iz
@@ -518,7 +518,7 @@
                 acc[i] = acc[i] + fold(a * b)
         return tuple(acc)
 
-    acc = lax.fori_loop(0, nz, products, tuple([jnp.zeros((8, LANES), F32)] * 6))
+    acc = lax.fori_loop(0, nz, products, tuple([jnp.zeros((8, LANES), F32)] * 6), unroll=2)
     sub8 = lax.broadcasted_iota(jnp.int32, (8, LANES), 0)
     packed = jnp.zeros((8, LANES), F32)
     for i in range(6):

time: 43.8 us -> 41.5 us (0.947)
  Pallas kernels: 42.8 us -> 40.6 us
    pallas_call x1, Pallas kernels: 38.8 us -> 36.5 us  [per_device(): pl.pallas_call(functools.partial(body, ngx, ngy, ngz, cap, epochs), out_s...]
where the time goes in v3:
time: 41.5 us; the launch traced here: 41.2 us
  Pallas kernels  40.6 us (98%)
  between operations  0.64 us (2%)
    pallas_call x1, Pallas kernels, per_device(): pl.pallas_call(functools.partial(body, ngx, ngy, ngz, cap, epochs), out_s...  36.5 us
    pallas_call x1, Pallas kernels, per_device(): pl.pallas_call(combine, out_shape=[field, field], in_specs=[smem, vmem, v...  4.01 us

profile of v3, /device:TPU:0, one launch (start us, length us, event | category | flops | bytes accessed | tf_op | source)
XLA Modules:
  0.0 41.2 jit_solution(15633509915476382739)
XLA Ops:
  0.6 36.5 %shard_map.122 = (f32[3,16,32,128]{3,2,1,0:T(8,128)}, f32[3,16,32,128]{3,2,1,0:T(8,128)}, f32[3,16,32,128]{3,2,1,0:T(8,128)}, f32[3,32,128]{2,1,0:T(8,128)}, f32[8,128]{1,0:T(8,128)}) custom-call(s32[64]{0:T(128)} %choice.1, f32[16]{0:T(128)} %depth.3, f32[4,3]{1,0:T(4,128)} %look.1, s32[1,64]{1,0:T(1,128)} %bitcast.3, s32[1,64]{1,0:T(1,128)} %bitcast.4, ...), custom_call_target="tpu_custom_call" | custom-call | tf_op jit(solution)/shard_map/pallas_call | solution.py:661
  37.2 4.0 %shard_map.123 = (f32[3,16,32,128]{3,2,1,0:T(8,128)}, f32[3,16,32,128]{3,2,1,0:T(8,128)}) custom-call(f32[16]{0:T(128)} %depth.3, f32[8,128]{1,0:T(8,128)} %get-tuple-element.7.coef, f32[3,32,128]{2,1,0:T(8,128)} %get-tuple-element.8.surf, f32[3,16,32,128]{3,2,1,0:T(8,128)} %get-tuple-element.9.v1_in, f32[3,16,32,128]{3,2,1,0:T(8,128)} %get-tuple-element.10.v2_in, ...), custom_call_target="tpu_custom_call" | custom-call | tf_op jit(solution)/shard_map/pallas_call | solution.py:713
